TPU v7x, 32 devices: a whole 2x2x4 slice. The times are simulated.
32 devices in a mesh: grp: 2 (over y), seq: 16 (over z, x, core).
Axes of the slice: x: 2, y: 2, z: 4, core: 2. Of those that a mesh axis runs over, the one named last changes fastest.
Arguments:
- history: bfloat16 [8192, 1024], P(('grp', 'seq')), parts along dimension 0, may hold values from -6 to 6
- candidates: bfloat16 [512, 1024], P(('grp', 'seq')), parts along dimension 0, may hold values from -6 to 6
- lengths: int32 [8], P('grp'), parts along dimension 0, may hold values from 1 to 2048, 4096 in all
- cand_user: int32 [512], P(('grp', 'seq')), parts along dimension 0, may hold values from 0 to 3
- w_in: bfloat16 [1, 1024, 4096], replicated, may hold values from -0.125 to 0.125
- w_out: bfloat16 [1, 1024, 1024], replicated, may hold values from -0.1875 to 0.1875
Outputs:
- history_out: bfloat16 [8192, 1024], P(('grp', 'seq')), parts along dimension 0
- cand_out: bfloat16 [512, 1024], P(('grp', 'seq')), parts along dimension 0
There are 2 independent parts, one for each index of `grp`. A program takes and returns all parts, laid end to end along the dimension named above; an argument that names none is the same for every part. Nothing has to cross between parts.
Inputs may be any that keep to these rules, and one draw needn't show every extreme that they name: Each user's history length is at least 1; the lengths sum to 4096, and one of them is exactly 2048.
All inputs are finite; a program needn't handle non-finite values.
Results may differ from a plain program's by a relative error of at most 0.0075.
Values may be sent and summed in bfloat16 or wider, within the bound.
A program may use at most 128 MiB of HBM per device.

v0:
```python
import functools

import jax
import jax.numpy as jnp
from jax import lax
from jax.experimental import pallas as pl
from jax.experimental.pallas import tpu as pltpu
from jax.sharding import PartitionSpec as P

HEADS = 8
WIN = 8
CHUNKS = 4
ROW = 4

eps = 1e-06
bf16 = jnp.bfloat16
f32 = jnp.float32


def layer_norm(rows):
    centred = rows - jnp.mean(rows, axis=-1, keepdims=True)
    return centred * lax.rsqrt(jnp.mean(centred * centred, axis=-1, keepdims=True) + eps)


def silu_of_twice(half):
    return half + half * jnp.tanh(half)


def dot(a, b):
    return jnp.dot(a, b, preferred_element_type=f32)


def dot_t(a, b):
    return lax.dot_general(a, b, (((1,), (1,)), ((), ())), preferred_element_type=f32)


def kernel(
    n,
    lengths,
    hist,
    cand,
    users_row,
    w_in_hbm,
    w_out_hbm,
    out_ref,
    cout_ref,
    w_in,
    w_out,
    wnd,
    q_s,
    u_s,
    kv_s,
    own_kv,
    acc,
    cbuf,
    ubuf,
    qc_s,
    part,
    buf1,
    buf2,
    buf3,
    out2,
    out3,
    users,
    uc_s,
    w_sem,
    x_send,
    x_recv,
    cz_send,
    cz_recv,
    uz_send,
    uz_recv,
    cx_send,
    cx_recv,
    rz_send,
    rz_recv,
):
    rows, width = hist.shape
    cr = cand.shape[0]
    head_dim = width // HEADS
    half_scale = 0.5 * head_dim ** (-0.5)
    depth = n // ROW
    s = lax.axis_index("seq")
    z = s // ROW
    r = s % ROW
    p = r // 2
    k = r % 2
    piece = rows // CHUNKS
    sibling = s + 1 - 2 * k
    partner = s + 2 - 4 * p

    w_copies = [
        pltpu.make_async_copy(
            w_in_hbm.at[0, :, pl.ds(c * width, width)], w_in.at[c], w_sem.at[c]
        )
        for c in range(4)
    ]
    w_copies.append(pltpu.make_async_copy(w_out_hbm.at[0], w_out, w_sem.at[4]))
    for c in (2, 3, 1, 0, 4):
        w_copies[c].start()

    eye = lax.broadcasted_iota(jnp.int32, (cr, cr), 0) == lax.broadcasted_iota(jnp.int32, (cr, cr), 1)
    column = jnp.sum(jnp.where(eye, users_row[...], 0), axis=1, keepdims=True)
    users[...] = jnp.broadcast_to(column, users.shape)

    barrier = pltpu.get_barrier_semaphore()
    pl.semaphore_signal(barrier, inc=1, device_id={"seq": sibling}, device_id_type=pl.DeviceIdType.MESH)
    pl.semaphore_signal(barrier, inc=1, device_id={"seq": partner}, device_id_type=pl.DeviceIdType.MESH)

    def greet(d, carry):
        pl.semaphore_signal(
            barrier,
            inc=1,
            device_id={"seq": (s + ROW * d) % n},
            device_id_type=pl.DeviceIdType.MESH,
        )
        return carry

    lax.fori_loop(1, depth, greet, 0)
    own_slot = 2 * ROW + r
    normed = layer_norm(hist[...].astype(f32)).astype(bf16)
    wnd[own_slot] = normed
    pl.semaphore_wait(barrier, depth + 1)

    def remote(src, dst, send, recv, to):
        return pltpu.make_async_remote_copy(
            src_ref=src,
            dst_ref=dst,
            send_sem=send,
            recv_sem=recv,
            device_id={"seq": to},
            device_id_type=pl.DeviceIdType.MESH,
        )

    def x_copy(src_slot, dst_slot, h, kind, to):
        part_rows = pl.ds(h * piece, piece)
        return remote(wnd.at[src_slot, part_rows], wnd.at[dst_slot, part_rows], x_send.at[kind, h], x_recv.at[dst_slot, h], to)

    up = (s + ROW) % n

    me_block = k * 2 + p

    def cz_copy(d, which):
        to = (s + ROW * d) % n
        at = pl.ds(pl.multiple_of(z * cr, cr), cr)
        if which == 0:
            return remote(cand, cbuf.at[me_block, at], cz_send.at[d], cz_recv.at[d], to)
        return remote(users, ubuf.at[me_block, at], uz_send.at[d], uz_recv.at[d], to)

    def cz_start(d, carry):
        cz_copy(d, 0).start()
        cz_copy(d, 1).start()
        return carry

    lax.fori_loop(1, depth, cz_start, 0)

    for h in range(CHUNKS):

        @pl.when(z + 1 < depth)
        def _():
            x_copy(own_slot, ROW + r, h, 0, up).start()

        if h == 0:

            @pl.when(p == 0)
            def _():
                x_copy(own_slot, own_slot, h, 1, partner).start()

        @pl.when(k == 0)
        def _():
            x_copy(own_slot, own_slot, h, 2, sibling).start()

    ends = []
    total = jnp.int32(0)
    for j in range(lengths.shape[0]):
        total = total + lengths[j]
        ends.append(total)

    def seg(pos):
        out = jnp.zeros(pos.shape, jnp.int32)
        for e in ends:
            out = out + (pos >= e).astype(jnp.int32)
        return out

    q_pos = s * rows + lax.broadcasted_iota(jnp.int32, (rows, 1), 0)
    q_seg = seg(q_pos)

    def project(normed, block):
        return silu_of_twice(dot(normed, w_in[block]) * 0.5).astype(bf16)

    def attend(kv, shard):
        k_pos = shard * rows + lax.broadcasted_iota(jnp.int32, (1, rows), 1)
        ok = (k_pos <= q_pos) & (q_pos - k_pos < (WIN - 1) * rows) & (seg(k_pos) == q_seg)
        for h in range(HEADS):
            cols = slice(h * head_dim, (h + 1) * head_dim)
            half = dot_t(q_s[:, cols], kv[0, :, cols]) * half_scale
            weight = jnp.where(ok, silu_of_twice(half), 0.0).astype(bf16)
            acc[:, cols] += dot(weight, kv[1, :, cols])

    def needed(slot, of):
        return (slot > of) & (slot < 2 * ROW + of) & (z - 2 + slot // ROW >= 0)

    def pair_of(j):
        base = 2 * ROW - ROW * (j // 2)
        swap = min(j // 2, 1) * p if isinstance(j, int) else jnp.minimum(j // 2, 1) * p
        return base + 2 * ((j + swap) % 2)

    def hop(j, h):
        mine = pair_of(j) + k
        pieces = pl.ds(h * piece, piece)
        came = [p == 1, None, z >= 1, z >= 1, (z >= 2) & (k == 1), (z >= 2) & (p == 0)][j]

        @pl.when(came)
        def _():
            pltpu.make_async_copy(hist.at[pieces], wnd.at[mine, pieces], x_recv.at[mine, h]).wait()
            if j == 2:

                @pl.when((z + 1 < depth) & (k == 1))
                def _():
                    x_copy(mine, mine - ROW, h, 3, up).start()

                x_copy(mine, mine, h, 4, partner).start()
            if j == 3:

                @pl.when((z + 1 < depth) & (r == 0))
                def _():
                    x_copy(mine, mine - ROW, h, 11, up).start()

            if j == 4:

                @pl.when(p == 1)
                def _():
                    x_copy(mine, mine, h, 5, partner).start()

            @pl.when(needed(mine, r + 1 - 2 * k))
            def _():
                x_copy(mine, mine, h, (6, None, 7, 8, 9, 10)[j], sibling).start()

    def all_hops(j, first):
        for h in range(first, CHUNKS):
            hop(j, h)

    acc[...] = jnp.zeros_like(acc)
    mine_at = pl.ds(pl.multiple_of(z * cr, cr), cr)
    cbuf[me_block, mine_at] = cand[...]
    ubuf[me_block, mine_at] = users[...]
    w_copies[2].wait()
    q_s[...] = project(normed, 2)
    w_copies[3].wait()
    own_kv[0] = project(normed, 3)
    w_copies[1].wait()
    own_kv[1] = project(normed, 1)

    def cz_wait(d, carry):
        cz_copy(d, 0).wait_recv()
        cz_copy(d, 1).wait_recv()
        return carry

    lax.fori_loop(1, depth, cz_wait, 0)
    to_partner = [
        remote(cbuf.at[me_block], cbuf.at[me_block], cx_send.at[0], cx_recv.at[0], partner),
        remote(ubuf.at[me_block], ubuf.at[me_block], cx_send.at[1], cx_recv.at[1], partner),
    ]
    for c in to_partner:
        c.start()
    for h in range(1, CHUNKS):

        @pl.when(p == 0)
        def _():
            x_copy(own_slot, own_slot, h, 1, partner).start()

    hop(2, 0)
    w_copies[0].wait()
    u_s[...] = project(normed, 0)
    attend(own_kv, s)
    hop(2, 1)
    for c in to_partner:
        c.wait_recv()
    to_sibling = [
        remote(cbuf.at[pl.ds(2 * k, 2)], cbuf.at[pl.ds(2 * k, 2)], cx_send.at[2], cx_recv.at[2], sibling),
        remote(ubuf.at[pl.ds(2 * k, 2)], ubuf.at[pl.ds(2 * k, 2)], cx_send.at[3], cx_recv.at[3], sibling),
    ]
    for c in to_sibling:
        c.start()
    u_c = project(layer_norm(cand[...].astype(f32)).astype(bf16), 0)
    uc_s[...] = u_c
    hop(2, 2)
    for c in to_sibling:
        c.wait_recv()

    def red1():
        return remote(part.at[pl.ds(2 - 2 * k, 2)], buf1, cx_send.at[4], cx_recv.at[4], sibling)

    def red2():
        return remote(out2, buf2, cx_send.at[5], cx_recv.at[5], partner)

    def red3(d):
        to_row = (z + d) % depth
        src = out3.at[pl.ds(pl.multiple_of(to_row * cr, cr), cr)]
        return remote(src, buf3.at[d], rz_send.at[d], rz_recv.at[d], (s + ROW * d) % n)

    block_rows = depth * cr
    k_row = s * rows + lax.broadcasted_iota(jnp.int32, (1, rows), 1)
    k_seg = seg(k_row)

    def cand_scores(first, count):
        size = count * block_rows
        c_norm = layer_norm(cbuf[pl.ds(first, count)].reshape(size, width).astype(f32)).astype(bf16)
        qc_s[...] = project(c_norm, 2)
        owner = ubuf[pl.ds(first, count)].reshape(size, ubuf.shape[-1])[:, :1]
        ok = owner == k_seg
        for h in range(HEADS):
            cols = slice(h * head_dim, (h + 1) * head_dim)
            half = dot_t(qc_s[:, cols], own_kv[0, :, cols]) * half_scale
            weight = jnp.where(ok, silu_of_twice(half), 0.0).astype(bf16)
            part[pl.ds(first, count), :, cols] = dot(weight, own_kv[1, :, cols]).reshape(
                count, block_rows, head_dim
            )

    count = qc_s.shape[0] // block_rows
    if count == ROW:
        cand_scores(0, ROW)
    else:

        def cand_block(b, carry):
            cand_scores(b * count, count)
            return carry

        lax.fori_loop(0, ROW // count, cand_block, 0)
    red1().start()

    def sums_across():
        red1().wait_recv()
        part[pl.ds(2 * k, 2)] += buf1[...]
        out2[...] = part[k * 2 + 1 - p].astype(bf16)
        red2().start()

    def sums_up():
        red2().wait_recv()
        part[me_block] += buf2[...].astype(f32)
        out3[...] = part[me_block].astype(bf16)

        def send(d, c):
            red3(d).start()
            return c

        lax.fori_loop(1, depth, send, 0)

    def event(e):
        if e == 0:
            hop(2, 3)
        if e == 1:
            sums_across()
        if e == 2:
            all_hops(0, 0)
        if e == 7:
            sums_up()
        for j, h in {2: ((3, 0),), 3: ((3, 1), (4, 0)), 4: ((3, 2), (4, 1)), 5: ((3, 3), (4, 2)), 6: ((4, 3),), 7: ((5, 0),), 8: ((5, 1),), 9: ((5, 2),), 10: ((5, 3),)}.get(e, ()):
            hop(j, h)

    def one(e, carry):
        for at in (0, 1, 2, 3, 4, 5, 6, 7, 8, 9, 10):

            @pl.when(e == at)
            def _():
                event(at)

        step = e // 2
        late = jnp.minimum(step // 3, 1)
        j = (1 - late) * ((step + 2) % 3) + late * step
        m = e % 2
        slot = pair_of(j) + (k + m) % 2

        @pl.when(needed(slot, r))
        def _():
            @pl.when(m == 1)
            def _():
                for h in range(CHUNKS):
                    pieces = pl.ds(h * piece, piece)
                    pltpu.make_async_copy(
                        hist.at[pieces], wnd.at[slot, pieces], x_recv.at[slot, h]
                    ).wait()

            norm = wnd[slot]
            kv_s[0] = project(norm, 3)
            kv_s[1] = project(norm, 1)
            attend(kv_s, (z - 2) * ROW + slot)

        return carry

    lax.fori_loop(0, 12, one, 0)

    w_copies[4].wait()

    def take(d, c):
        red3(d).wait_recv()
        return c + buf3[d].astype(f32)

    cattn = lax.fori_loop(1, depth, take, part[me_block, mine_at])
    y_c = (layer_norm(cattn) * uc_s[...].astype(f32)).astype(bf16)
    y = (layer_norm(acc[...]) * u_s[...].astype(f32)).astype(bf16)
    both = dot(jnp.concatenate([y, y_c], axis=0), w_out[...])
    out_ref[...] = (hist[...].astype(f32) + both[:rows]).astype(bf16)
    cout_ref[...] = (cand[...].astype(f32) + both[rows:]).astype(bf16)

    for c in to_partner + to_sibling + [red1(), red2()]:
        c.wait_send()

    def left(d, c):
        cz_copy(d, 0).wait_send()
        cz_copy(d, 1).wait_send()
        red3(d).wait_send()
        return c

    lax.fori_loop(1, depth, left, 0)
    for h in range(CHUNKS):

        @pl.when(z + 1 < depth)
        def _():
            x_copy(own_slot, ROW + r, h, 0, up).wait_send()

        @pl.when(p == 0)
        def _():
            x_copy(own_slot, own_slot, h, 1, partner).wait_send()

        @pl.when(k == 0)
        def _():
            x_copy(own_slot, own_slot, h, 2, sibling).wait_send()

        @pl.when((z >= 1) & (z + 1 < depth) & (k == 1))
        def _():
            x_copy(ROW + r, r, h, 3, up).wait_send()

        @pl.when(z >= 1)
        def _():
            x_copy(ROW + r, ROW + r, h, 4, partner).wait_send()

        @pl.when((z >= 2) & (r == 3))
        def _():
            x_copy(r, r, h, 5, partner).wait_send()

        other = r + 1 - 2 * k
        across = 2 * (1 - p) + k

        @pl.when((z >= 1) & (z + 1 < depth) & (r == 0))
        def _():
            x_copy(ROW + across, across, h, 11, up).wait_send()

        for kind, came, slot in (
            (6, p == 1, 2 * ROW + k),
            (7, z >= 1, ROW + r),
            (8, z >= 1, ROW + across),
            (9, (z >= 2) & (k == 1), r),
            (10, (z >= 2) & (p == 0), across),
        ):

            @pl.when(came & needed(slot, other))
            def _():
                x_copy(slot, slot, h, kind, sibling).wait_send()


def per_device(n, history, candidates, lengths, cand_user, w_in, w_out):
    rows, width = history.shape
    cr = candidates.shape[0]
    depth = n // ROW
    users = cand_user[None, :]
    vmem = pl.BlockSpec(memory_space=pltpu.VMEM)
    dma = pltpu.SemaphoreType.DMA
    block = depth * cr
    many = ROW * block if ROW * block <= 512 else block
    return pl.pallas_call(
        functools.partial(kernel, n),
        out_shape=(
            jax.ShapeDtypeStruct((rows, width), bf16),
            jax.ShapeDtypeStruct((cr, width), bf16),
        ),
        in_specs=[
            pl.BlockSpec(memory_space=pltpu.SMEM),
            vmem,
            vmem,
            vmem,
            pl.BlockSpec(memory_space=pl.ANY),
            pl.BlockSpec(memory_space=pl.ANY),
        ],
        out_specs=(vmem, vmem),
        scratch_shapes=[
            pltpu.VMEM((4, width, width), bf16),
            pltpu.VMEM((width, width), bf16),
            pltpu.VMEM((3 * ROW, rows, width), bf16),
            pltpu.VMEM((rows, width), bf16),
            pltpu.VMEM((rows, width), bf16),
            pltpu.VMEM((2, rows, width), bf16),
            pltpu.VMEM((2, rows, width), bf16),
            pltpu.VMEM((rows, width), f32),
            pltpu.VMEM((ROW, block, width), bf16),
            pltpu.VMEM((ROW, block, 128), jnp.int32),
            pltpu.VMEM((many, width), bf16),
            pltpu.VMEM((ROW, block, width), f32),
            pltpu.VMEM((2, block, width), f32),
            pltpu.VMEM((block, width), bf16),
            pltpu.VMEM((depth, cr, width), bf16),
            pltpu.VMEM((block, width), bf16),
            pltpu.VMEM((block, width), bf16),
            pltpu.VMEM((cr, 128), jnp.int32),
            pltpu.VMEM((cr, width), bf16),
            dma((5,)),
            dma((12, CHUNKS)),
            dma((3 * ROW, CHUNKS)),
            dma((depth,)),
            dma((depth,)),
            dma((depth,)),
            dma((depth,)),
            dma((6,)),
            dma((6,)),
            dma((depth,)),
            dma((depth,)),
        ],
        compiler_params=pltpu.CompilerParams(
            collective_id=0, has_side_effects=True, vmem_limit_bytes=60 * 1024 * 1024
        ),
    )(lengths, history, candidates, users, w_in, w_out)


def solution(mesh):
    n = mesh.shape["seq"]
    placed = (
        P(("grp", "seq"), None),
        P(("grp", "seq"), None),
        P("grp"),
        P(("grp", "seq")),
        P(),
        P(),
    )
    return jax.shard_map(
        functools.partial(per_device, n),
        mesh=mesh,
        in_specs=placed,
        out_specs=(P(("grp", "seq"), None), P(("grp", "seq"), None)),
        check_vma=False,
    )
```

profile of v0, /device:TPU:6, one launch (start us, length us, event | category | flops | bytes accessed | tf_op | source)
XLA Modules:
  0.0 47.5 jit_solution(16268611951426830219)
XLA Ops:
  0.6 43.6 %shard_map.77 = (bf16[256,1024]{1,0:T(8,128)(2,1)}, bf16[16,1024]{1,0:T(8,128)(2,1)}) custom-call(s32[4]{0:T(128)} %lengths.1, bf16[256,1024]{1,0:T(8,128)(2,1)} %hist.1, bf16[16,1024]{1,0:T(8,128)(2,1)} %cand.1, s32[1,16]{1,0:T(1,128)} %bitcast.1, bf16[1,1024,4096]{2,1,0:T(8,128)(2,1)} %w_in_hbm.1, bf16[1,1024,1024]{2,1,0:T(8,128)(2,1)} %w_out_hbm.1), custom_call_target="tpu_custom_call" | custom-call | tf_op jit(solution)/shard_map/pallas_call | solution.py:471
  44.3 1.9 %copy.10 = bf16[256,1024]{1,0:T(8,128)(2,1)} copy(bf16[256,1024]{1,0:T(8,128)(2,1)} %get-tuple-element.4) | data formatting | bytes 1048576
  46.2 1.4 %copy.11 = bf16[16,1024]{1,0:T(8,128)(2,1)} copy(bf16[16,1024]{1,0:T(8,128)(2,1)} %get-tuple-element.5) | data formatting | bytes 65536
where the time goes:
time: 47.8 us; the launch traced here: 47.5 us
  Pallas kernels  43.6 us (91%)
  local copies, waits for them, and re-layouts  3.24 us (7%)
  between operations  0.64 us (1%)
    pallas_call x1, Pallas kernels, per_device(): pl.pallas_call(functools.partial(kernel, n), out_shape=(jax.ShapeDtypeStr...  43.6 us
    unnamed x2, local copies, waits for them, and re-layouts  3.24 us

commit v1 on v0

v1 whole, which is shorter than its diff:
```python
import functools

import jax
import jax.numpy as jnp
from jax import lax
from jax.experimental import pallas as pl
from jax.experimental.pallas import tpu as pltpu
from jax.sharding import PartitionSpec as P

HEADS = 8
WIN = 8
PIECES = 4
ROW = 4
SIB = 6
B1, B2, B3, B4, B5 = 0, 1, 2, 3, 4

eps = 1e-06
bf16 = jnp.bfloat16
f32 = jnp.float32


def layer_norm(rows):
    centred = rows - jnp.mean(rows, axis=-1, keepdims=True)
    return centred * lax.rsqrt(jnp.mean(centred * centred, axis=-1, keepdims=True) + eps)


def silu_of_twice(half):
    return half + half * jnp.tanh(half)


def dot(a, b):
    return jnp.dot(a, b, preferred_element_type=f32)


def dot_t(a, b):
    return lax.dot_general(a, b, (((1,), (1,)), ((), ())), preferred_element_type=f32)


def pick(i, entries):
    out = 0
    for at, value in entries.items():
        out = out + value * (1 - jnp.minimum((i - at) * (i - at), 1))
    return out


def kernel(
    n,
    lengths,
    hist,
    cand,
    users_row,
    w_in_hbm,
    w_out_hbm,
    out_ref,
    cout_ref,
    w_in,
    w_out,
    own,
    xb,
    kv,
    q_s,
    u_s,
    acc,
    cmsg,
    cbuf,
    qc_s,
    part,
    buf1,
    out3,
    buf3,
    fin,
    cfin,
    w_sem,
    x_send,
    x_recv,
    kv_send,
    kv_recv,
    c_send,
    c_recv,
    up_send,
    down_send,
    rz_send,
    rz_recv,
):
    rows, width = hist.shape
    cr = cand.shape[0]
    head_dim = width // HEADS
    half_scale = 0.5 * head_dim ** (-0.5)
    depth = n // ROW
    s = lax.axis_index("seq")
    z = s // ROW
    r = s % ROW
    p = r // 2
    k = r % 2
    piece = rows // PIECES
    sibling = s + 1 - 2 * k
    partner = s + 2 - 4 * p
    above = (s + ROW) % n
    below = (s + n - ROW) % n
    has_above = z + 1 < depth
    has_below = z >= 1

    w_copies = [
        pltpu.make_async_copy(
            w_in_hbm.at[0, :, pl.ds(c * width, width)], w_in.at[c], w_sem.at[c]
        )
        for c in range(4)
    ]
    w_copies.append(pltpu.make_async_copy(w_out_hbm.at[0], w_out, w_sem.at[4]))
    for c in (3, 1, 2, 0, 4):
        w_copies[c].start()

    barrier = pltpu.get_barrier_semaphore()

    def greet(to):
        pl.semaphore_signal(barrier, inc=1, device_id={"seq": to}, device_id_type=pl.DeviceIdType.MESH)

    peers = (
        (None, sibling),
        (None, partner),
        (has_above, above),
        (has_below, below),
        (has_above & (k == 1), (s + 3) % n),
        (has_below & (k == 0), (s + n - 3) % n),
        (r == 1, (s + 1) % n),
        (r == 2, (s + n - 1) % n),
    )
    for cond, to in peers:
        if cond is None:
            greet(to)
        else:
            pl.when(cond)(functools.partial(greet, to))

    eye = lax.broadcasted_iota(jnp.int32, (cr, cr), 0) == lax.broadcasted_iota(jnp.int32, (cr, cr), 1)
    column = jnp.sum(jnp.where(eye, users_row[...], 0), axis=1, keepdims=True)
    c_normed = layer_norm(cand[...].astype(f32)).astype(bf16)
    cmsg[:, :width] = c_normed
    cmsg[:, width:] = jnp.broadcast_to(column, (cr, 128)).astype(f32).astype(bf16)

    @pl.when(p == 1)
    def _():
        cbuf[k, z, pl.ds(cr, cr)] = cmsg[...]

    normed = layer_norm(hist[...].astype(f32)).astype(bf16)
    own[...] = normed
    pl.semaphore_wait(barrier, sum(1 if cond is None else cond.astype(jnp.int32) for cond, _ in peers))

    def remote(src, dst, send, recv, to):
        return pltpu.make_async_remote_copy(
            src_ref=src,
            dst_ref=dst,
            send_sem=send,
            recv_sem=recv,
            device_id={"seq": to},
            device_id_type=pl.DeviceIdType.MESH,
        )

    def x_copy(src, dst, h, kind, to):
        at = pl.ds(h * piece, piece)
        return remote(src.at[at], xb.at[dst, at], x_send.at[kind, h], x_recv.at[dst, h], to)

    moves = (
        (0, own, B2, above, has_above, None),
        (1, own, B1, partner, p == 0, None),
        (2, xb.at[B2], B3, partner, has_below, B2),
        (3, xb.at[B2], B5, (s + 3) % n, has_below & has_above & (k == 1), B2),
        (4, xb.at[B3], B4, above, has_below & has_above & (r == 0), B3),
        (5, xb.at[B5], B4, (s + n - 1) % n, (z >= 2) & (r == 2), B5),
    )
    arrives = {
        B1: p == 1,
        B2: has_below,
        B3: has_below,
        B4: (z >= 2) & (p == 0),
        B5: (z >= 2) & (k == 0),
    }

    def c_cross():
        return remote(cmsg, cbuf.at[k, z, pl.ds(0, cr)], c_send.at[0], c_recv.at[depth], partner)

    def c_block(block, send, to):
        return remote(cbuf.at[k, block], cbuf.at[k, block], send, c_recv.at[block], to)

    def c_swap():
        return remote(cbuf.at[k], cbuf.at[k], c_send.at[1], c_recv.at[depth + 1], sibling)

    @pl.when(p == 0)
    def _():
        c_cross().start()

    for h in range(PIECES):
        for kind, src, dst, to, cond, _ in moves[:2]:

            @pl.when(cond)
            def _():
                x_copy(src, dst, h, kind, to).start()

    def hop(buf, h):
        at = pl.ds(h * piece, piece)

        @pl.when(arrives[buf])
        def _():
            pltpu.make_async_copy(hist.at[at], xb.at[buf, at], x_recv.at[buf, h]).wait()
            for kind, src, dst, to, cond, source in moves:
                if source == buf:

                    @pl.when(cond)
                    def _():
                        x_copy(src, dst, h, kind, to).start()

    ends = []
    total = jnp.int32(0)
    for j in range(lengths.shape[0]):
        total = total + lengths[j]
        ends.append(total)

    def seg(pos):
        out = jnp.zeros(pos.shape, jnp.int32)
        for e in ends:
            out = out + (pos >= e).astype(jnp.int32)
        return out

    q_pos = s * rows + lax.broadcasted_iota(jnp.int32, (rows, 1), 0)
    q_seg = seg(q_pos)

    def project(normed, block):
        return silu_of_twice(dot(normed, w_in[block]) * 0.5).astype(bf16)

    def swap_copy(t):
        return remote(kv.at[t], kv.at[SIB + t], kv_send.at[t], kv_recv.at[t], sibling)

    def shard_of(t, kk):
        ahead = pick(t, {1: ROW * z + kk, 2: ROW * (z - 1) + 2 * p + kk, 3: ROW * (z - 1) + 2 - 2 * p + kk})
        return ahead + pick(t, {0: ROW * z + 2 * p + kk, 4: ROW * (z - 2) + 2 + kk, 5: ROW * (z - 2) + 1 + 2 * p})

    def attend(a):
        side = a // SIB
        t = a % SIB
        shard = shard_of(t, k + side - 2 * k * side)
        k_pos = shard * rows + lax.broadcasted_iota(jnp.int32, (1, rows), 1)
        ok = (k_pos <= q_pos) & (q_pos - k_pos < (WIN - 1) * rows) & (seg(k_pos) == q_seg)
        for h in range(HEADS):
            cols = slice(h * head_dim, (h + 1) * head_dim)
            half = dot_t(q_s[:, cols], kv[a, 0, :, cols]) * half_scale
            weight = jnp.where(ok, silu_of_twice(half), 0.0).astype(bf16)
            acc[:, cols] += dot(weight, kv[a, 1, :, cols])

    w_copies[3].wait()
    kv[0, 0] = project(normed, 3)
    w_copies[1].wait()
    kv[0, 1] = project(normed, 1)

    @pl.when(k == 0)
    def _():
        swap_copy(0).start()

    def c_round(d):
        low = jnp.maximum(z - d, 0)
        high = jnp.minimum(z + d, depth - 1)
        if isinstance(d, int) and d == 0:
            pl.when(has_above)(lambda: c_block(z, up_send.at[d], above).start())
            pl.when(has_below)(lambda: c_block(z, down_send.at[d], below).start())
            return

        @pl.when(z - d >= 0)
        def _():
            c_block(low, up_send.at[d], above).wait_recv()
            pl.when(has_above)(lambda: c_block(low, up_send.at[d], above).start())

        @pl.when(z + d < depth)
        def _():
            c_block(high, down_send.at[d], below).wait_recv()
            pl.when(has_below)(lambda: c_block(high, down_send.at[d], below).start())

    def c_first():
        remote(cmsg, cbuf.at[k, z, pl.ds(0, cr)], c_send.at[0], c_recv.at[depth], partner).wait_recv()
        c_round(0)

    pl.when(p == 1)(c_first)
    w_copies[2].wait()
    q_s[...] = project(normed, 2)
    w_copies[0].wait()
    u_s[...] = project(jnp.concatenate([normed, c_normed], axis=0), 0)
    acc[...] = jnp.zeros_like(acc)
    if depth > 1:
        pl.when(p == 1)(functools.partial(c_round, 1))

    block_rows = part.shape[1]
    k_seg = seg(s * rows + lax.broadcasted_iota(jnp.int32, (1, rows), 1)).astype(f32)
    kk_seg = seg((ROW * z + k) * rows + lax.broadcasted_iota(jnp.int32, (1, rows), 1)).astype(f32)
    group = qc_s.shape[1]
    groups = 2 * block_rows // group
    lines = group // (2 * cr)

    def c_queries():
        def one(b, carry):
            if groups == 1:
                x = cbuf[:, :, :, :width].reshape(group, width)
            else:
                per = groups // 2
                x = cbuf[b // per, pl.ds(b % per * lines, lines), :, :width].reshape(group, width)
            qc_s[b] = project(x, 2)
            return carry

        lax.fori_loop(0, groups, one, 0)

    def c_attend(t, segs):
        def one(b, carry):
            per = max(groups // 2, 1)
            if groups == 1:
                owner = cbuf[:, :, :, width:].reshape(group, 128)[:, :1]
            else:
                owner = cbuf[b // per, pl.ds(b % per * lines, lines), :, width:].reshape(group, 128)[:, :1]
            ok = owner.astype(f32) == segs
            for h in range(HEADS):
                cols = slice(h * head_dim, (h + 1) * head_dim)
                half = dot_t(qc_s[b, :, cols], kv[t, 0, :, cols]) * half_scale
                weight = jnp.where(ok, silu_of_twice(half), 0.0).astype(bf16)
                value = dot(weight, kv[t, 1, :, cols])
                if groups == 1:
                    value = value.reshape(2, block_rows, head_dim)
                    if t:
                        value = value + part[:, :, cols]
                    part[:, :, cols] = value
                else:
                    at = pl.ds(pl.multiple_of(b % per * group, group), group)
                    if t:
                        value = value + part[b // per, at, cols]
                    part[b // per, at, cols] = value
            return carry

        lax.fori_loop(0, groups, one, 0)

    def red1():
        return remote(part.at[1 - k], buf1, c_send.at[2], c_recv.at[depth + 2], sibling)

    def red3(d):
        return remote(out3.at[(z + d) % depth], buf3.at[d], rz_send.at[d], rz_recv.at[d], (s + ROW * d) % n)

    def red4():
        return remote(fin, cfin, c_send.at[3], c_recv.at[depth + 3], partner)

    def c_middle():
        def rest(d, carry):
            c_round(d)
            return carry

        lax.fori_loop(3, depth, rest, 0)
        c_swap().start()
        c_swap().wait_recv()
        c_queries()
        c_attend(0, k_seg)

    def c_late():
        c_attend(1, kk_seg)
        red1().start()

    def c_sums():
        red1().wait_recv()
        part[k] += buf1[...]
        out3[...] = part[k].astype(bf16).reshape(out3.shape)

        def send(d, c):
            red3(d).start()
            return c

        lax.fori_loop(1, depth, send, 0)

    def c_done():
        mine = part[k, pl.ds(pl.multiple_of(z * 2 * cr, 2 * cr), 2 * cr)]

        def take(d, c):
            red3(d).wait_recv()
            return c + buf3[d].astype(f32)

        mine = lax.fori_loop(1, depth, take, mine)
        fin[...] = mine[:cr]
        red4().start()
        cfin[...] = mine[cr:]

    def event(e):
        if e == 1:
            hop(B2, 0)
            if depth > 2:
                pl.when(p == 1)(functools.partial(c_round, 2))
        if e == 2:
            hop(B2, 1)
            pl.when(p == 1)(c_middle)
            hop(B2, 2)
            hop(B2, 3)
            for h in range(PIECES):
                hop(B1, h)

            pl.when(p == 0)(functools.partial(hop, B3, 0))
            pl.when(p == 0)(functools.partial(hop, B3, 1))
        if e == 3:
            pl.when(p == 0)(functools.partial(hop, B3, 2))
            pl.when(p == 1)(functools.partial(hop, B5, 0))
        if e == 4:
            pl.when(p == 0)(functools.partial(hop, B3, 3))
            pl.when(p == 1)(functools.partial(hop, B5, 1))
            pl.when(p == 1)(functools.partial(hop, B5, 2))
        if e == 5:
            pl.when(p == 1)(functools.partial(hop, B5, 3))
            pl.when(p == 1)(c_late)
        if e == 6:
            pl.when(p == 1)(c_sums)
        if e == 7:
            for h in range(PIECES):
                pl.when(p == 0)(functools.partial(hop, B4, h))
        if e == 8:
            for h in range(PIECES):
                pl.when(p == 1)(functools.partial(hop, B3, h))
                pl.when(p == 0)(functools.partial(hop, B5, h))
        if e == 9:
            pl.when(p == 1)(c_done)

    proj_at = {2: (2, 1), 3: (0, 2), 5: (3, 0), 7: (4, 5), 8: (5, 3)}
    att_at = {
        0: (1, 1),
        1: (1 + SIB, 1 + SIB),
        3: (1 + 2, 1 + 1),
        4: (1 + SIB + 2, 1 + SIB + 1),
        5: (1 + 3, 1 + 2),
        6: (1 + SIB + 3, 1 + SIB + 2),
        7: (0, 1 + 5),
        8: (1 + 5, 1 + 3),
        9: (1 + 4, 1 + SIB + 3),
        10: (1 + SIB + 4, 0),
    }

    def mix(table):
        return {at: v0 * (1 - p) + v1 * p for at, (v0, v1) in table.items()}

    proj_table, att_table = mix(proj_at), mix(att_at)

    def one(e, carry):
        for at in range(11):

            @pl.when(e == at)
            def _():
                event(at)

        t = pick(e, proj_table)

        @pl.when((t > 0) & (z >= t // 2) & ((t < 5) | (k == 0)))
        def _():
            x = xb[t - jnp.minimum(t, 1)]
            kv[t, 0] = project(x, 3)
            kv[t, 1] = project(x, 1)
            pl.when(t < 5)(lambda: swap_copy(t).start())

        a = pick(e, att_table) - 1
        ta = (a + SIB) % SIB
        side = (a + SIB) // SIB - 1

        @pl.when((a >= 0) & (z >= ta // 2) & ((ta < 5) | (k == 0)) & ((ta > 0) | (side < 1) | (k == 1)))
        def _():
            pl.when(side == 1)(lambda: swap_copy(ta).wait_recv())
            attend(a)

        return carry

    lax.fori_loop(0, 11, one, 0)

    w_copies[4].wait()

    @pl.when(p == 0)
    def _():
        red4().wait_recv()

    y_c = (layer_norm(cfin[...]) * u_s[pl.ds(rows, cr)].astype(f32)).astype(bf16)
    y = (layer_norm(acc[...]) * u_s[pl.ds(0, rows)].astype(f32)).astype(bf16)
    both = dot(jnp.concatenate([y, y_c], axis=0), w_out[...])
    out_ref[...] = (hist[...].astype(f32) + both[:rows]).astype(bf16)
    cout_ref[...] = (cand[...].astype(f32) + both[rows:]).astype(bf16)

    for h in range(PIECES):
        for kind, src, dst, to, cond, _ in moves:

            @pl.when(cond)
            def _():
                x_copy(src, dst, h, kind, to).wait_send()

    for t, cond in ((0, k == 0), (1, p == 1), (2, z >= 1), (3, z >= 1), (4, (z >= 2) & (p == 0))):

        @pl.when(cond)
        def _():
            swap_copy(t).wait_send()

    pl.when(p == 0)(lambda: c_cross().wait_send())

    @pl.when(p == 1)
    def _():
        c_swap().wait_send()
        red1().wait_send()
        red4().wait_send()

        def left(d, c):
            pl.when(has_above & (z - d >= 0))(lambda: c_block(0, up_send.at[d], above).wait_send())
            pl.when(has_below & (z + d < depth))(lambda: c_block(0, down_send.at[d], below).wait_send())
            return c

        lax.fori_loop(0, depth, left, 0)

        def sums(d, c):
            red3(d).wait_send()
            return c

        lax.fori_loop(1, depth, sums, 0)


def per_device(n, history, candidates, lengths, cand_user, w_in, w_out):
    rows, width = history.shape
    cr = candidates.shape[0]
    depth = n // ROW
    users = cand_user[None, :]
    vmem = pl.BlockSpec(memory_space=pltpu.VMEM)
    dma = pltpu.SemaphoreType.DMA
    block = depth * 2 * cr
    group = 2 * block if 2 * block <= 256 else min(block, 256)
    return pl.pallas_call(
        functools.partial(kernel, n),
        out_shape=(
            jax.ShapeDtypeStruct((rows, width), bf16),
            jax.ShapeDtypeStruct((cr, width), bf16),
        ),
        in_specs=[
            pl.BlockSpec(memory_space=pltpu.SMEM),
            vmem,
            vmem,
            vmem,
            pl.BlockSpec(memory_space=pl.ANY),
            pl.BlockSpec(memory_space=pl.ANY),
        ],
        out_specs=(vmem, vmem),
        scratch_shapes=[
            pltpu.VMEM((4, width, width), bf16),
            pltpu.VMEM((width, width), bf16),
            pltpu.VMEM((rows, width), bf16),
            pltpu.VMEM((5, rows, width), bf16),
            pltpu.VMEM((SIB + 5, 2, rows, width), bf16),
            pltpu.VMEM((rows, width), bf16),
            pltpu.VMEM((rows + cr, width), bf16),
            pltpu.VMEM((rows, width), f32),
            pltpu.VMEM((cr, width + 128), bf16),
            pltpu.VMEM((2, depth, 2 * cr, width + 128), bf16),
            pltpu.VMEM((2 * block // group, group, width), bf16),
            pltpu.VMEM((2, block, width), f32),
            pltpu.VMEM((block, width), f32),
            pltpu.VMEM((depth, 2 * cr, width), bf16),
            pltpu.VMEM((depth, 2 * cr, width), bf16),
            pltpu.VMEM((cr, width), f32),
            pltpu.VMEM((cr, width), f32),
            dma((5,)),
            dma((6, PIECES)),
            dma((5, PIECES)),
            dma((5,)),
            dma((5,)),
            dma((4,)),
            dma((depth + 4,)),
            dma((depth,)),
            dma((depth,)),
            dma((depth,)),
            dma((depth,)),
        ],
        compiler_params=pltpu.CompilerParams(
            collective_id=0, has_side_effects=True, vmem_limit_bytes=60 * 1024 * 1024
        ),
    )(lengths, history, candidates, users, w_in, w_out)


def solution(mesh):
    n = mesh.shape["seq"]
    placed = (
        P(("grp", "seq"), None),
        P(("grp", "seq"), None),
        P("grp"),
        P(("grp", "seq")),
        P(),
        P(),
    )
    return jax.shard_map(
        functools.partial(per_device, n),
        mesh=mesh,
        in_specs=placed,
        out_specs=(P(("grp", "seq"), None), P(("grp", "seq"), None)),
        check_vma=False,
    )
```

time: 47.8 us -> 53.8 us (1.13)
  the two profiles are of different devices: /device:TPU:6 before, /device:TPU:0 now
where the time goes in v1:
time: 53.8 us; the launch traced here: 53.3 us
  Pallas kernels  49.4 us (92%)
  local copies, waits for them, and re-layouts  3.24 us (6%)
  between operations  0.64 us (1%)
    pallas_call x1, Pallas kernels, per_device(): pl.pallas_call(functools.partial(kernel, n), out_shape=(jax.ShapeDtypeStr...  49.4 us
    unnamed x2, local copies, waits for them, and re-layouts  3.24 us

profile of v1, /device:TPU:0, one launch (start us, length us, event | category | flops | bytes accessed | tf_op | source)
XLA Modules:
  0.0 53.3 jit_solution(5947438990091630055)
XLA Ops:
  0.6 49.4 %shard_map.77 = (bf16[256,1024]{1,0:T(8,128)(2,1)}, bf16[16,1024]{1,0:T(8,128)(2,1)}) custom-call(s32[4]{0:T(128)} %lengths.1, bf16[256,1024]{1,0:T(8,128)(2,1)} %hist.1, bf16[16,1024]{1,0:T(8,128)(2,1)} %cand.1, s32[1,16]{1,0:T(1,128)} %bitcast.1, bf16[1,1024,4096]{2,1,0:T(8,128)(2,1)} %w_in_hbm.1, bf16[1,1024,1024]{2,1,0:T(8,128)(2,1)} %w_out_hbm.1), custom_call_target="tpu_custom_call" | custom-call | tf_op jit(solution)/shard_map/pallas_call | solution.py:522
  50.0 1.9 %copy.10 = bf16[256,1024]{1,0:T(8,128)(2,1)} copy(bf16[256,1024]{1,0:T(8,128)(2,1)} %get-tuple-element.4) | data formatting | bytes 1048576
  51.9 1.4 %copy.11 = bf16[16,1024]{1,0:T(8,128)(2,1)} copy(bf16[16,1024]{1,0:T(8,128)(2,1)} %get-tuple-element.5) | data formatting | bytes 65536

commit v2 on v1

--- a/solution.py
+++ b/solution.py
@@ -11,6 +11,7 @@
 WIN = 8
 PIECES = 4
 ROW = 4
+EARLY = 3
 SIB = 6
 B1, B2, B3, B4, B5 = 0, 1, 2, 3, 4
 
@@ -52,7 +53,6 @@
     w_in_hbm,
     w_out_hbm,
     out_ref,
-    cout_ref,
     w_in,
     w_out,
     own,
@@ -65,11 +65,8 @@
     cbuf,
     qc_s,
     part,
-    buf1,
     out3,
     buf3,
-    fin,
-    cfin,
     w_sem,
     x_send,
     x_recv,
@@ -139,7 +136,7 @@
 
     @pl.when(p == 1)
     def _():
-        cbuf[k, z, pl.ds(cr, cr)] = cmsg[...]
+        cbuf[z, pl.ds(cr, cr)] = cmsg[...]
 
     normed = layer_norm(hist[...].astype(f32)).astype(bf16)
     own[...] = normed
@@ -163,7 +160,7 @@
         (0, own, B2, above, has_above, None),
         (1, own, B1, partner, p == 0, None),
         (2, xb.at[B2], B3, partner, has_below, B2),
-        (3, xb.at[B2], B5, (s + 3) % n, has_below & has_above & (k == 1), B2),
+        (3, xb.at[B2], B5, (s + 3) % n, has_below & has_above & (k == 1), None),
         (4, xb.at[B3], B4, above, has_below & has_above & (r == 0), B3),
         (5, xb.at[B5], B4, (s + n - 1) % n, (z >= 2) & (r == 2), B5),
     )
@@ -176,24 +173,26 @@
     }
 
     def c_cross():
-        return remote(cmsg, cbuf.at[k, z, pl.ds(0, cr)], c_send.at[0], c_recv.at[depth], partner)
+        return remote(cmsg, cbuf.at[z, pl.ds(0, cr)], c_send.at[0], c_recv.at[depth], partner)
 
     def c_block(block, send, to):
-        return remote(cbuf.at[k, block], cbuf.at[k, block], send, c_recv.at[block], to)
-
-    def c_swap():
-        return remote(cbuf.at[k], cbuf.at[k], c_send.at[1], c_recv.at[depth + 1], sibling)
+        return remote(cbuf.at[block], cbuf.at[block], send, c_recv.at[block], to)
 
     @pl.when(p == 0)
     def _():
         c_cross().start()
 
+    def send(which, first, last, also=None):
+        kind, src, dst, to, cond, _ = moves[which]
+
+        @pl.when(cond if also is None else cond & also)
+        def _():
+            for h in range(first, last):
+                x_copy(src, dst, h, kind, to).start()
+
     for h in range(PIECES):
-        for kind, src, dst, to, cond, _ in moves[:2]:
-
-            @pl.when(cond)
-            def _():
-                x_copy(src, dst, h, kind, to).start()
+        send(0, h, h + 1, None if h < EARLY else p == 0)
+        send(1, h, h + 1)
 
     def hop(buf, h):
         at = pl.ds(h * piece, piece)
@@ -250,7 +249,7 @@
     w_copies[1].wait()
     kv[0, 1] = project(normed, 1)
 
-    @pl.when(k == 0)
+    @pl.when((k == 0) | (p == 1))
     def _():
         swap_copy(0).start()
 
@@ -273,160 +272,121 @@
             pl.when(has_below)(lambda: c_block(high, down_send.at[d], below).start())
 
     def c_first():
-        remote(cmsg, cbuf.at[k, z, pl.ds(0, cr)], c_send.at[0], c_recv.at[depth], partner).wait_recv()
+        c_cross().wait_recv()
         c_round(0)
 
-    pl.when(p == 1)(c_first)
     w_copies[2].wait()
     q_s[...] = project(normed, 2)
     w_copies[0].wait()
     u_s[...] = project(jnp.concatenate([normed, c_normed], axis=0), 0)
     acc[...] = jnp.zeros_like(acc)
-    if depth > 1:
-        pl.when(p == 1)(functools.partial(c_round, 1))
-
-    block_rows = part.shape[1]
-    k_seg = seg(s * rows + lax.broadcasted_iota(jnp.int32, (1, rows), 1)).astype(f32)
-    kk_seg = seg((ROW * z + k) * rows + lax.broadcasted_iota(jnp.int32, (1, rows), 1)).astype(f32)
-    group = qc_s.shape[1]
-    groups = 2 * block_rows // group
+    pl.when(p == 1)(c_first)
+    send(0, EARLY, EARLY + 1, p == 1)
+
+    group = part.shape[1]
     lines = group // (2 * cr)
 
-    def c_queries():
-        def one(b, carry):
-            if groups == 1:
-                x = cbuf[:, :, :, :width].reshape(group, width)
-            else:
-                per = groups // 2
-                x = cbuf[b // per, pl.ds(b % per * lines, lines), :, :width].reshape(group, width)
-            qc_s[b] = project(x, 2)
-            return carry
-
-        lax.fori_loop(0, groups, one, 0)
-
-    def c_attend(t, segs):
-        def one(b, carry):
-            per = max(groups // 2, 1)
-            if groups == 1:
-                owner = cbuf[:, :, :, width:].reshape(group, 128)[:, :1]
-            else:
-                owner = cbuf[b // per, pl.ds(b % per * lines, lines), :, width:].reshape(group, 128)[:, :1]
-            ok = owner.astype(f32) == segs
-            for h in range(HEADS):
-                cols = slice(h * head_dim, (h + 1) * head_dim)
-                half = dot_t(qc_s[b, :, cols], kv[t, 0, :, cols]) * half_scale
-                weight = jnp.where(ok, silu_of_twice(half), 0.0).astype(bf16)
-                value = dot(weight, kv[t, 1, :, cols])
-                if groups == 1:
-                    value = value.reshape(2, block_rows, head_dim)
-                    if t:
-                        value = value + part[:, :, cols]
-                    part[:, :, cols] = value
-                else:
-                    at = pl.ds(pl.multiple_of(b % per * group, group), group)
-                    if t:
-                        value = value + part[b // per, at, cols]
-                    part[b // per, at, cols] = value
-            return carry
-
-        lax.fori_loop(0, groups, one, 0)
-
-    def red1():
-        return remote(part.at[1 - k], buf1, c_send.at[2], c_recv.at[depth + 2], sibling)
-
-    def red3(d):
-        return remote(out3.at[(z + d) % depth], buf3.at[d], rz_send.at[d], rz_recv.at[d], (s + ROW * d) % n)
-
-    def red4():
-        return remote(fin, cfin, c_send.at[3], c_recv.at[depth + 3], partner)
-
-    def c_middle():
+    def c_last():
         def rest(d, carry):
             c_round(d)
             return carry
 
         lax.fori_loop(3, depth, rest, 0)
-        c_swap().start()
-        c_swap().wait_recv()
-        c_queries()
-        c_attend(0, k_seg)
-
-    def c_late():
-        c_attend(1, kk_seg)
-        red1().start()
-
-    def c_sums():
-        red1().wait_recv()
-        part[k] += buf1[...]
-        out3[...] = part[k].astype(bf16).reshape(out3.shape)
+
+    def c_scores():
+        pl.when(k == 0)(lambda: swap_copy(0).wait_recv())
+
+        def one(b, carry):
+            at = pl.ds(pl.multiple_of(b * lines, lines), lines)
+            qc_s[...] = project(cbuf[at, :, :width].reshape(group, width), 2)
+            owner = cbuf[at, :, width:].reshape(group, 128)[:, :1].astype(f32)
+            part[b] = jnp.zeros((group, width), f32)
+
+            def shard(i, carry):
+                t = i // 2
+                side = i % 2
+                a = t + side * SIB
+                near = shard_of(t, k + side - 2 * k * side)
+                ok = owner == seg(near * rows + lax.broadcasted_iota(jnp.int32, (1, rows), 1)).astype(f32)
+                for h in range(HEADS):
+                    cols = slice(h * head_dim, (h + 1) * head_dim)
+                    half = dot_t(qc_s[:, cols], kv[a, 0, :, cols]) * half_scale
+                    weight = jnp.where(ok, silu_of_twice(half), 0.0).astype(bf16)
+                    part[b, :, cols] += dot(weight, kv[a, 1, :, cols])
+                return carry
+
+            lax.fori_loop(0, 4, shard, 0)
+            out3[at] = part[b].astype(bf16).reshape(lines, 2 * cr, width)
+            return carry
+
+        lax.fori_loop(0, depth // lines, one, 0)
 
         def send(d, c):
-            red3(d).start()
+            for side in range(2):
+                red(d, side).start()
             return c
 
         lax.fori_loop(1, depth, send, 0)
-
-    def c_done():
-        mine = part[k, pl.ds(pl.multiple_of(z * 2 * cr, 2 * cr), 2 * cr)]
-
-        def take(d, c):
-            red3(d).wait_recv()
-            return c + buf3[d].astype(f32)
-
-        mine = lax.fori_loop(1, depth, take, mine)
-        fin[...] = mine[:cr]
-        red4().start()
-        cfin[...] = mine[cr:]
+        red(0, 0).start()
+
+    def red(d, side):
+        src = out3.at[(z + d) % depth, pl.ds(side * cr, cr)]
+        return remote(src, buf3.at[d], rz_send.at[side, d], rz_recv.at[d], (ROW * (z + d) + 2 * side + k) % n)
+
+    def red_wait(d):
+        return remote(out3.at[0, pl.ds(0, cr)], buf3.at[d], rz_send.at[0, d], rz_recv.at[d], partner).wait_recv()
+
+    def only(side, f, *a):
+        pl.when(p == side)(functools.partial(f, *a))
 
     def event(e):
         if e == 1:
             hop(B2, 0)
-            if depth > 2:
-                pl.when(p == 1)(functools.partial(c_round, 2))
         if e == 2:
-            hop(B2, 1)
-            pl.when(p == 1)(c_middle)
-            hop(B2, 2)
-            hop(B2, 3)
+            for h in range(1, PIECES):
+                hop(B2, h)
             for h in range(PIECES):
                 hop(B1, h)
-
-            pl.when(p == 0)(functools.partial(hop, B3, 0))
-            pl.when(p == 0)(functools.partial(hop, B3, 1))
+            if depth > 1:
+                only(1, c_round, 1)
+            send(3, 0, PIECES // 2)
+            only(0, send, 3, PIECES // 2, PIECES)
+            only(0, hop, B3, 0)
+            only(0, hop, B3, 1)
         if e == 3:
-            pl.when(p == 0)(functools.partial(hop, B3, 2))
-            pl.when(p == 1)(functools.partial(hop, B5, 0))
+            if depth > 2:
+                only(1, c_round, 2)
+            only(1, send, 3, PIECES // 2, PIECES)
+            only(0, hop, B3, 2)
+            only(0, hop, B3, 3)
         if e == 4:
-            pl.when(p == 0)(functools.partial(hop, B3, 3))
-            pl.when(p == 1)(functools.partial(hop, B5, 1))
-            pl.when(p == 1)(functools.partial(hop, B5, 2))
+            only(1, c_last)
+            only(1, hop, B5, 0)
+            only(1, hop, B5, 1)
         if e == 5:
-            pl.when(p == 1)(functools.partial(hop, B5, 3))
-            pl.when(p == 1)(c_late)
+            only(1, hop, B5, 2)
+            only(1, hop, B5, 3)
+            only(1, c_scores)
         if e == 6:
-            pl.when(p == 1)(c_sums)
+            for h in range(PIECES):
+                only(0, hop, B4, h)
         if e == 7:
             for h in range(PIECES):
-                pl.when(p == 0)(functools.partial(hop, B4, h))
-        if e == 8:
-            for h in range(PIECES):
-                pl.when(p == 1)(functools.partial(hop, B3, h))
-                pl.when(p == 0)(functools.partial(hop, B5, h))
-        if e == 9:
-            pl.when(p == 1)(c_done)
-
-    proj_at = {2: (2, 1), 3: (0, 2), 5: (3, 0), 7: (4, 5), 8: (5, 3)}
+                only(1, hop, B3, h)
+                only(0, hop, B5, h)
+
+    proj_at = {2: (2, 1), 3: (3, 2), 6: (4, 5), 7: (5, 3)}
     att_at = {
         0: (1, 1),
         1: (1 + SIB, 1 + SIB),
-        3: (1 + 2, 1 + 1),
-        4: (1 + SIB + 2, 1 + SIB + 1),
-        5: (1 + 3, 1 + 2),
-        6: (1 + SIB + 3, 1 + SIB + 2),
-        7: (0, 1 + 5),
-        8: (1 + 5, 1 + 3),
-        9: (1 + 4, 1 + SIB + 3),
-        10: (1 + SIB + 4, 0),
+        2: (1 + 2, 1 + 1),
+        3: (1 + SIB + 2, 1 + SIB + 1),
+        4: (1 + 3, 1 + 2),
+        5: (1 + SIB + 3, 1 + SIB + 2),
+        6: (0, 1 + 5),
+        7: (1 + 5, 1 + 3),
+        8: (1 + 4, 1 + SIB + 3),
+        9: (1 + SIB + 4, 0),
     }
 
     def mix(table):
@@ -435,7 +395,7 @@
     proj_table, att_table = mix(proj_at), mix(att_at)
 
     def one(e, carry):
-        for at in range(11):
+        for at in range(10):
 
             @pl.when(e == at)
             def _():
@@ -461,19 +421,28 @@
 
         return carry
 
-    lax.fori_loop(0, 11, one, 0)
+    lax.fori_loop(0, 10, one, 0)
 
     w_copies[4].wait()
+
+    def take(d, c):
+        red_wait(d)
+        return c + buf3[d].astype(f32)
 
     @pl.when(p == 0)
     def _():
-        red4().wait_recv()
-
-    y_c = (layer_norm(cfin[...]) * u_s[pl.ds(rows, cr)].astype(f32)).astype(bf16)
+        red_wait(0)
+
+    @pl.when(p == 1)
+    def _():
+        buf3[0] = out3[z, pl.ds(cr, cr)]
+
+    cattn = lax.fori_loop(1, depth, take, buf3[0].astype(f32))
+    y_c = (layer_norm(cattn) * u_s[pl.ds(rows, cr)].astype(f32)).astype(bf16)
     y = (layer_norm(acc[...]) * u_s[pl.ds(0, rows)].astype(f32)).astype(bf16)
     both = dot(jnp.concatenate([y, y_c], axis=0), w_out[...])
-    out_ref[...] = (hist[...].astype(f32) + both[:rows]).astype(bf16)
-    cout_ref[...] = (cand[...].astype(f32) + both[rows:]).astype(bf16)
+    out_ref[pl.ds(0, rows)] = (hist[...].astype(f32) + both[:rows]).astype(bf16)
+    out_ref[pl.ds(rows, cr)] = (cand[...].astype(f32) + both[rows:]).astype(bf16)
 
     for h in range(PIECES):
         for kind, src, dst, to, cond, _ in moves:
@@ -482,7 +451,7 @@
             def _():
                 x_copy(src, dst, h, kind, to).wait_send()
 
-    for t, cond in ((0, k == 0), (1, p == 1), (2, z >= 1), (3, z >= 1), (4, (z >= 2) & (p == 0))):
+    for t, cond in ((0, (k == 0) | (p == 1)), (1, p == 1), (2, z >= 1), (3, z >= 1), (4, (z >= 2) & (p == 0))):
 
         @pl.when(cond)
         def _():
@@ -492,9 +461,7 @@
 
     @pl.when(p == 1)
     def _():
-        c_swap().wait_send()
-        red1().wait_send()
-        red4().wait_send()
+        red(0, 0).wait_send()
 
         def left(d, c):
             pl.when(has_above & (z - d >= 0))(lambda: c_block(0, up_send.at[d], above).wait_send())
@@ -504,10 +471,26 @@
         lax.fori_loop(0, depth, left, 0)
 
         def sums(d, c):
-            red3(d).wait_send()
+            for side in range(2):
+                red(d, side).wait_send()
             return c
 
         lax.fori_loop(1, depth, sums, 0)
+
+
+def hand_out(both, out_ref, cout_ref, held, sem):
+    rows, cr = out_ref.shape[0], cout_ref.shape[0]
+    parts = (pl.ds(0, rows), pl.ds(rows, cr))
+    to = (out_ref, cout_ref)
+    loads = [pltpu.make_async_copy(both.at[at], held.at[at], sem.at[i]) for i, at in enumerate(parts)]
+    saves = [pltpu.make_async_copy(held.at[at], to[i], sem.at[i]) for i, at in enumerate(parts)]
+    for c in loads:
+        c.start()
+    for i in range(2):
+        loads[i].wait()
+        saves[i].start()
+    for c in saves:
+        c.wait()
 
 
 def per_device(n, history, candidates, lengths, cand_user, w_in, w_out):
@@ -518,13 +501,10 @@
     vmem = pl.BlockSpec(memory_space=pltpu.VMEM)
     dma = pltpu.SemaphoreType.DMA
     block = depth * 2 * cr
-    group = 2 * block if 2 * block <= 256 else min(block, 256)
-    return pl.pallas_call(
+    group = min(block, 256)
+    both = pl.pallas_call(
         functools.partial(kernel, n),
-        out_shape=(
-            jax.ShapeDtypeStruct((rows, width), bf16),
-            jax.ShapeDtypeStruct((cr, width), bf16),
-        ),
+        out_shape=jax.ShapeDtypeStruct((rows + cr, width), bf16),
         in_specs=[
             pl.BlockSpec(memory_space=pltpu.SMEM),
             vmem,
@@ -533,7 +513,7 @@
             pl.BlockSpec(memory_space=pl.ANY),
             pl.BlockSpec(memory_space=pl.ANY),
         ],
-        out_specs=(vmem, vmem),
+        out_specs=vmem,
         scratch_shapes=[
             pltpu.VMEM((4, width, width), bf16),
             pltpu.VMEM((width, width), bf16),
@@ -544,30 +524,38 @@
             pltpu.VMEM((rows + cr, width), bf16),
             pltpu.VMEM((rows, width), f32),
             pltpu.VMEM((cr, width + 128), bf16),
-            pltpu.VMEM((2, depth, 2 * cr, width + 128), bf16),
-            pltpu.VMEM((2 * block // group, group, width), bf16),
-            pltpu.VMEM((2, block, width), f32),
-            pltpu.VMEM((block, width), f32),
+            pltpu.VMEM((depth, 2 * cr, width + 128), bf16),
+            pltpu.VMEM((group, width), bf16),
+            pltpu.VMEM((block // group, group, width), f32),
             pltpu.VMEM((depth, 2 * cr, width), bf16),
-            pltpu.VMEM((depth, 2 * cr, width), bf16),
-            pltpu.VMEM((cr, width), f32),
-            pltpu.VMEM((cr, width), f32),
+            pltpu.VMEM((depth, cr, width), bf16),
             dma((5,)),
             dma((6, PIECES)),
             dma((5, PIECES)),
             dma((5,)),
             dma((5,)),
-            dma((4,)),
-            dma((depth + 4,)),
+            dma((1,)),
+            dma((depth + 1,)),
             dma((depth,)),
             dma((depth,)),
-            dma((depth,)),
+            dma((2, depth)),
             dma((depth,)),
         ],
         compiler_params=pltpu.CompilerParams(
             collective_id=0, has_side_effects=True, vmem_limit_bytes=60 * 1024 * 1024
         ),
     )(lengths, history, candidates, users, w_in, w_out)
+    hbm = pl.BlockSpec(memory_space=pl.ANY)
+    return pl.pallas_call(
+        hand_out,
+        out_shape=(
+            jax.ShapeDtypeStruct((rows, width), bf16),
+            jax.ShapeDtypeStruct((cr, width), bf16),
+        ),
+        in_specs=[hbm],
+        out_specs=(hbm, hbm),
+        scratch_shapes=[pltpu.VMEM((rows + cr, width), bf16), dma((2,))],
+    )(both)
 
 
 def solution(mesh):

time: 53.8 us -> 44.8 us (0.83)
  the two profiles are of different devices: /device:TPU:0 before, /device:TPU:24 now
where the time goes in v2:
time: 44.8 us; the launch traced here: 44.7 us
  Pallas kernels  44 us (98%)
  between operations  0.64 us (1%)
    pallas_call x1, Pallas kernels, per_device(): pl.pallas_call(functools.partial(kernel, n), out_shape=jax.ShapeDtypeStru...  42.2 us
    pallas_call x1, Pallas kernels, per_device(): pl.pallas_call(hand_out, out_shape=(jax.ShapeDtypeStruct((rows, width), b...  1.85 us

profile of v2, /device:TPU:24, one launch (start us, length us, event | category | flops | bytes accessed | tf_op | source)
XLA Modules:
  0.0 44.7 jit_solution(6714854874083519543)
XLA Ops:
  0.6 42.2 %shard_map.77.both = bf16[272,1024]{1,0:T(8,128)(2,1)} custom-call(s32[4]{0:T(128)} %lengths.1, bf16[256,1024]{1,0:T(8,128)(2,1)} %hist.1, bf16[16,1024]{1,0:T(8,128)(2,1)} %cand.1, s32[1,16]{1,0:T(1,128)} %bitcast.1, bf16[1,1024,4096]{2,1,0:T(8,128)(2,1)} %w_in_hbm.1, bf16[1,1024,1024]{2,1,0:T(8,128)(2,1)} %w_out_hbm.1), custom_call_target="tpu_custom_call" | custom-call | tf_op jit(solution)/shard_map/pallas_call | solution.py:505
  42.8 1.9 %shard_map.78 = (bf16[256,1024]{1,0:T(8,128)(2,1)}, bf16[16,1024]{1,0:T(8,128)(2,1)}) custom-call(bf16[272,1024]{1,0:T(8,128)(2,1)} %shard_map.77.both), custom_call_target="tpu_custom_call" | custom-call | tf_op jit(solution)/shard_map/pallas_call | solution.py:549

commit v3 on v2

--- a/solution.py
+++ b/solution.py
@@ -46,13 +46,18 @@
 
 def kernel(
     n,
+    lengths_hbm,
+    hist_hbm,
+    cand_hbm,
+    users_hbm,
+    w_in_hbm,
+    w_out_hbm,
+    out_ref,
     lengths,
     hist,
     cand,
     users_row,
-    w_in_hbm,
-    w_out_hbm,
-    out_ref,
+    in_sem,
     w_in,
     w_out,
     own,
@@ -97,6 +102,14 @@
     has_above = z + 1 < depth
     has_below = z >= 1
 
+    in_copies = [
+        pltpu.make_async_copy(src, dst, in_sem.at[i])
+        for i, (src, dst) in enumerate(
+            ((hist_hbm, hist), (cand_hbm, cand), (users_hbm, users_row), (lengths_hbm, lengths))
+        )
+    ]
+    for c in in_copies:
+        c.start()
     w_copies = [
         pltpu.make_async_copy(
             w_in_hbm.at[0, :, pl.ds(c * width, width)], w_in.at[c], w_sem.at[c]
@@ -104,9 +117,6 @@
         for c in range(4)
     ]
     w_copies.append(pltpu.make_async_copy(w_out_hbm.at[0], w_out, w_sem.at[4]))
-    for c in (3, 1, 2, 0, 4):
-        w_copies[c].start()
-
     barrier = pltpu.get_barrier_semaphore()
 
     def greet(to):
@@ -117,10 +127,8 @@
         (None, partner),
         (has_above, above),
         (has_below, below),
-        (has_above & (k == 1), (s + 3) % n),
-        (has_below & (k == 0), (s + n - 3) % n),
-        (r == 1, (s + 1) % n),
-        (r == 2, (s + n - 1) % n),
+        (has_above & (r == 1), (s + 3) % n),
+        (has_below & (r == 0), (s + n - 3) % n),
     )
     for cond, to in peers:
         if cond is None:
@@ -128,6 +136,11 @@
         else:
             pl.when(cond)(functools.partial(greet, to))
 
+    for c in (3, 1, 2, 0, 4):
+        w_copies[c].start()
+    for c in in_copies[1:]:
+        c.wait()
+
     eye = lax.broadcasted_iota(jnp.int32, (cr, cr), 0) == lax.broadcasted_iota(jnp.int32, (cr, cr), 1)
     column = jnp.sum(jnp.where(eye, users_row[...], 0), axis=1, keepdims=True)
     c_normed = layer_norm(cand[...].astype(f32)).astype(bf16)
@@ -138,8 +151,18 @@
     def _():
         cbuf[z, pl.ds(cr, cr)] = cmsg[...]
 
+    in_copies[0].wait()
     normed = layer_norm(hist[...].astype(f32)).astype(bf16)
     own[...] = normed
+
+    @pl.when((p == 1) & (z == 0))
+    def _():
+        xb[B2] = jnp.zeros((rows, width), bf16)
+
+    @pl.when((p == 1) & (k == 0) & (z == 1))
+    def _():
+        xb[B5] = jnp.zeros((rows, width), bf16)
+
     pl.semaphore_wait(barrier, sum(1 if cond is None else cond.astype(jnp.int32) for cond, _ in peers))
 
     def remote(src, dst, send, recv, to):
@@ -160,16 +183,17 @@
         (0, own, B2, above, has_above, None),
         (1, own, B1, partner, p == 0, None),
         (2, xb.at[B2], B3, partner, has_below, B2),
-        (3, xb.at[B2], B5, (s + 3) % n, has_below & has_above & (k == 1), None),
+        (3, xb.at[B2], B5, (s + 3 + p) % n, has_below & has_above & (k == 1), None),
         (4, xb.at[B3], B4, above, has_below & has_above & (r == 0), B3),
-        (5, xb.at[B5], B4, (s + n - 1) % n, (z >= 2) & (r == 2), B5),
+        (5, xb.at[B5], B4, partner, (z >= 2) & (r == 3), B5),
+        (6, xb.at[B5], B5, sibling, (z >= 2) & (r == 3), B5),
     )
     arrives = {
         B1: p == 1,
         B2: has_below,
         B3: has_below,
         B4: (z >= 2) & (p == 0),
-        B5: (z >= 2) & (k == 0),
+        B5: (z >= 2) & ((k == 0) | (p == 1)),
     }
 
     def c_cross():
@@ -225,23 +249,48 @@
     def project(normed, block):
         return silu_of_twice(dot(normed, w_in[block]) * 0.5).astype(bf16)
 
+    half = rows // 2
+    low = pl.ds(0, half)
+    high = pl.ds(half, half)
+
     def swap_copy(t):
         return remote(kv.at[t], kv.at[SIB + t], kv_send.at[t], kv_recv.at[t], sibling)
 
-    def shard_of(t, kk):
-        ahead = pick(t, {1: ROW * z + kk, 2: ROW * (z - 1) + 2 * p + kk, 3: ROW * (z - 1) + 2 - 2 * p + kk})
-        return ahead + pick(t, {0: ROW * z + 2 * p + kk, 4: ROW * (z - 2) + 2 + kk, 5: ROW * (z - 2) + 1 + 2 * p})
+    def swap_half(t):
+        to = low if t == 3 else high
+        return remote(kv.at[t, :, low], kv.at[SIB + 3, :, to], kv_send.at[t], kv_recv.at[t], sibling)
+
+    def bases(t, side):
+        kk = k + side - 2 * k * side
+        first = ROW * (z - 1 + p) + kk
+        second = ROW * (z - 1) + 2 + kk
+        late = ROW * (z - 2 + p) + 2 - 2 * p + kk
+        lone = ROW * (z - 2) + 1 + 2 * p
+        mine = s + side * (1 - 2 * k)
+        whole = k * (1 - side) + side
+        h = half
+        a = pick(t, {0: mine * rows, 1: first * rows, 2: first * rows + h, 3: late * rows, 4: late * rows + h})
+        b = pick(
+            t,
+            {
+                0: mine * rows + h,
+                1: second * rows,
+                2: second * rows + h,
+                3: (1 - whole) * lone * rows + whole * (late * rows + h),
+                4: lone * rows + h,
+            },
+        )
+        return a, b
 
     def attend(a):
-        side = a // SIB
-        t = a % SIB
-        shard = shard_of(t, k + side - 2 * k * side)
-        k_pos = shard * rows + lax.broadcasted_iota(jnp.int32, (1, rows), 1)
+        start, later = bases(a % SIB, a // SIB)
+        lane = lax.broadcasted_iota(jnp.int32, (1, rows), 1)
+        k_pos = jnp.where(lane < half, start + lane, later + lane - half)
         ok = (k_pos <= q_pos) & (q_pos - k_pos < (WIN - 1) * rows) & (seg(k_pos) == q_seg)
         for h in range(HEADS):
             cols = slice(h * head_dim, (h + 1) * head_dim)
-            half = dot_t(q_s[:, cols], kv[a, 0, :, cols]) * half_scale
-            weight = jnp.where(ok, silu_of_twice(half), 0.0).astype(bf16)
+            score = dot_t(q_s[:, cols], kv[a, 0, :, cols]) * half_scale
+            weight = jnp.where(ok, silu_of_twice(score), 0.0).astype(bf16)
             acc[:, cols] += dot(weight, kv[a, 1, :, cols])
 
     w_copies[3].wait()
@@ -296,27 +345,33 @@
     def c_scores():
         pl.when(k == 0)(lambda: swap_copy(0).wait_recv())
 
-        def one(b, carry):
-            at = pl.ds(pl.multiple_of(b * lines, lines), lines)
+        def one(g, carry):
+            at = pl.ds(pl.multiple_of(g * lines, lines), lines)
             qc_s[...] = project(cbuf[at, :, :width].reshape(group, width), 2)
             owner = cbuf[at, :, width:].reshape(group, 128)[:, :1].astype(f32)
-            part[b] = jnp.zeros((group, width), f32)
+            part[g] = jnp.zeros((group, width), f32)
 
             def shard(i, carry):
+                for at in (2, 3):
+                    pl.when((r == 3) & (g == 0) & (i == 2 * at - 3))(functools.partial(hop, B5, at))
                 t = i // 2
                 side = i % 2
                 a = t + side * SIB
-                near = shard_of(t, k + side - 2 * k * side)
+                b = 2 * t + side * SIB
+                rest = pl.ds(pl.multiple_of((1 - t) * half, half), half)
+                near = ROW * z + 2 - 2 * t + k + side - 2 * k * side
                 ok = owner == seg(near * rows + lax.broadcasted_iota(jnp.int32, (1, rows), 1)).astype(f32)
                 for h in range(HEADS):
                     cols = slice(h * head_dim, (h + 1) * head_dim)
-                    half = dot_t(qc_s[:, cols], kv[a, 0, :, cols]) * half_scale
-                    weight = jnp.where(ok, silu_of_twice(half), 0.0).astype(bf16)
-                    part[b, :, cols] += dot(weight, kv[a, 1, :, cols])
+                    keys = jnp.concatenate([kv[a, 0, low, cols], kv[b, 0, rest, cols]], axis=0)
+                    values = jnp.concatenate([kv[a, 1, low, cols], kv[b, 1, rest, cols]], axis=0)
+                    score = dot_t(qc_s[...][:, cols], keys) * half_scale
+                    weight = jnp.where(ok, silu_of_twice(score), 0.0).astype(bf16)
+                    part[g, :, cols] += dot(weight, values)
                 return carry
 
             lax.fori_loop(0, 4, shard, 0)
-            out3[at] = part[b].astype(bf16).reshape(lines, 2 * cr, width)
+            out3[at] = part[g].astype(bf16).reshape(lines, 2 * cr, width)
             return carry
 
         lax.fori_loop(0, depth // lines, one, 0)
@@ -337,65 +392,78 @@
         return remote(out3.at[0, pl.ds(0, cr)], buf3.at[d], rz_send.at[0, d], rz_recv.at[d], partner).wait_recv()
 
     def only(side, f, *a):
-        pl.when(p == side)(functools.partial(f, *a))
+        pl.when(p == side if side < 2 else r == side)(functools.partial(f, *a))
 
     def event(e):
         if e == 1:
             hop(B2, 0)
         if e == 2:
-            for h in range(1, PIECES):
-                hop(B2, h)
-            for h in range(PIECES):
+            hop(B2, 1)
+            only(0, hop, B2, 2)
+            for h in (0, 1):
                 hop(B1, h)
+                only(0, hop, B3, h)
+        if e == 3:
+            only(1, hop, B2, 2)
+            only(0, hop, B2, 3)
+            only(0, send, 3, 0, PIECES)
+        if e == 4:
+            only(1, hop, B2, 3)
+            for h in (2, 3):
+                hop(B1, h)
+                only(0, hop, B3, h)
             if depth > 1:
                 only(1, c_round, 1)
-            send(3, 0, PIECES // 2)
-            only(0, send, 3, PIECES // 2, PIECES)
-            only(0, hop, B3, 0)
-            only(0, hop, B3, 1)
-        if e == 3:
+            only(1, send, 3, 0, PIECES // 2)
+        if e == 5:
             if depth > 2:
-                only(1, c_round, 2)
+                only(3, c_round, 2)
             only(1, send, 3, PIECES // 2, PIECES)
-            only(0, hop, B3, 2)
-            only(0, hop, B3, 3)
-        if e == 4:
-            only(1, c_last)
-            only(1, hop, B5, 0)
-            only(1, hop, B5, 1)
-        if e == 5:
-            only(1, hop, B5, 2)
-            only(1, hop, B5, 3)
-            only(1, c_scores)
+            only(3, hop, B5, 0)
+            only(3, hop, B5, 1)
         if e == 6:
-            for h in range(PIECES):
+            only(3, c_last)
+            only(3, c_scores)
+            if depth > 2:
+                only(2, c_round, 2)
+            for h in (0, 1):
+                only(2, hop, B5, h)
+                only(1, hop, B3, h)
                 only(0, hop, B4, h)
+                only(0, hop, B5, h)
+            late(1)
         if e == 7:
-            for h in range(PIECES):
+            only(2, c_last)
+            only(2, c_scores)
+            late(0)
+
+    def late(core):
+        @pl.when(k == core)
+        def _():
+            for h in (2, 3):
+                only(2, hop, B5, h)
                 only(1, hop, B3, h)
+                only(0, hop, B4, h)
                 only(0, hop, B5, h)
 
-    proj_at = {2: (2, 1), 3: (3, 2), 6: (4, 5), 7: (5, 3)}
-    att_at = {
-        0: (1, 1),
-        1: (1 + SIB, 1 + SIB),
-        2: (1 + 2, 1 + 1),
-        3: (1 + SIB + 2, 1 + SIB + 1),
-        4: (1 + 3, 1 + 2),
-        5: (1 + SIB + 3, 1 + SIB + 2),
-        6: (0, 1 + 5),
-        7: (1 + 5, 1 + 3),
-        8: (1 + 4, 1 + SIB + 3),
-        9: (1 + SIB + 4, 0),
+    proj_table = {2: 1, 4: 2, 6: 3, 7: 4}
+    att_table = {
+        0: 1,
+        1: 1 + SIB,
+        2: 1 + 1,
+        3: 1 + SIB + 1,
+        4: 1 + 2,
+        5: 1 + SIB + 2,
+        6: 1 + 3,
+        7: 1 + 4,
+        8: 1 + SIB + 3,
     }
 
-    def mix(table):
-        return {at: v0 * (1 - p) + v1 * p for at, (v0, v1) in table.items()}
-
-    proj_table, att_table = mix(proj_at), mix(att_at)
+    def live(t):
+        return z >= jnp.minimum(t, 1) * (1 - p) + t // 3
 
     def one(e, carry):
-        for at in range(10):
+        for at in range(9):
 
             @pl.when(e == at)
             def _():
@@ -403,25 +471,40 @@
 
         t = pick(e, proj_table)
 
-        @pl.when((t > 0) & (z >= t // 2) & ((t < 5) | (k == 0)))
-        def _():
-            x = xb[t - jnp.minimum(t, 1)]
+        @pl.when((t > 0) & live(t) & ((t < 4) | (k == 0)))
+        def _():
+            end = t // 3
+            one_at = (1 - end) * (1 - p) + end * (3 - p)
+            two_at = (1 - end) * (2 - p) + end * (4 * (1 - k) + (3 - p) * k)
+            one_off = (t + 1) % 2
+            two_off = jnp.maximum(one_off, end * k)
+            x1 = xb[one_at, pl.ds(pl.multiple_of(one_off * half, half), half)]
+            x2 = xb[two_at, pl.ds(pl.multiple_of(two_off * half, half), half)]
+            x = jnp.concatenate([x1, x2], axis=0)
             kv[t, 0] = project(x, 3)
             kv[t, 1] = project(x, 1)
-            pl.when(t < 5)(lambda: swap_copy(t).start())
+            pl.when((t < 3) | ((t == 3) & (k == 1)))(lambda: swap_copy(t).start())
+            pl.when((t == 3) & (k == 0))(lambda: swap_half(3).start())
+            pl.when((t == 4) & (k == 0))(lambda: swap_half(4).start())
 
         a = pick(e, att_table) - 1
-        ta = (a + SIB) % SIB
-        side = (a + SIB) // SIB - 1
-
-        @pl.when((a >= 0) & (z >= ta // 2) & ((ta < 5) | (k == 0)) & ((ta > 0) | (side < 1) | (k == 1)))
-        def _():
-            pl.when(side == 1)(lambda: swap_copy(ta).wait_recv())
+        ta = a % SIB
+        side = a // SIB
+
+        @pl.when(live(ta) & ((ta < 4) | (k == 0)) & ((ta > 0) | (side < 1) | (k == 1)))
+        def _():
+            pl.when((side == 1) & ((ta < 3) | (k == 0)))(lambda: swap_copy(ta).wait_recv())
+
+            @pl.when((side == 1) & (ta == 3) & (k == 1))
+            def _():
+                swap_half(3).wait_recv()
+                swap_half(4).wait_recv()
+
             attend(a)
 
         return carry
 
-    lax.fori_loop(0, 10, one, 0)
+    lax.fori_loop(0, 9, one, 0)
 
     w_copies[4].wait()
 
@@ -451,11 +534,16 @@
             def _():
                 x_copy(src, dst, h, kind, to).wait_send()
 
-    for t, cond in ((0, (k == 0) | (p == 1)), (1, p == 1), (2, z >= 1), (3, z >= 1), (4, (z >= 2) & (p == 0))):
+    for t, cond in ((0, (k == 0) | (p == 1)), (1, live(1)), (2, live(2)), (3, live(3) & (k == 1))):
 
         @pl.when(cond)
         def _():
             swap_copy(t).wait_send()
+
+    @pl.when(live(3) & (k == 0))
+    def _():
+        swap_half(3).wait_send()
+        swap_half(4).wait_send()
 
     pl.when(p == 0)(lambda: c_cross().wait_send())
 
@@ -478,17 +566,13 @@
         lax.fori_loop(1, depth, sums, 0)
 
 
-def hand_out(both, out_ref, cout_ref, held, sem):
+def hand_out(both, out_ref, cout_ref, sem):
     rows, cr = out_ref.shape[0], cout_ref.shape[0]
     parts = (pl.ds(0, rows), pl.ds(rows, cr))
     to = (out_ref, cout_ref)
-    loads = [pltpu.make_async_copy(both.at[at], held.at[at], sem.at[i]) for i, at in enumerate(parts)]
-    saves = [pltpu.make_async_copy(held.at[at], to[i], sem.at[i]) for i, at in enumerate(parts)]
-    for c in loads:
+    saves = [pltpu.make_async_copy(both.at[at], to[i], sem.at[i]) for i, at in enumerate(parts)]
+    for c in saves:
         c.start()
-    for i in range(2):
-        loads[i].wait()
-        saves[i].start()
     for c in saves:
         c.wait()
 
@@ -505,16 +589,14 @@
     both = pl.pallas_call(
         functools.partial(kernel, n),
         out_shape=jax.ShapeDtypeStruct((rows + cr, width), bf16),
-        in_specs=[
-            pl.BlockSpec(memory_space=pltpu.SMEM),
-            vmem,
-            vmem,
-            vmem,
-            pl.BlockSpec(memory_space=pl.ANY),
-            pl.BlockSpec(memory_space=pl.ANY),
-        ],
+        in_specs=[pl.BlockSpec(memory_space=pltpu.HBM)] * 6,
         out_specs=vmem,
         scratch_shapes=[
+            pltpu.SMEM(lengths.shape, jnp.int32),
+            pltpu.VMEM((rows, width), bf16),
+            pltpu.VMEM((cr, width), bf16),
+            pltpu.VMEM((1, cr), jnp.int32),
+            dma((4,)),
             pltpu.VMEM((4, width, width), bf16),
             pltpu.VMEM((width, width), bf16),
             pltpu.VMEM((rows, width), bf16),
@@ -530,7 +612,7 @@
             pltpu.VMEM((depth, 2 * cr, width), bf16),
             pltpu.VMEM((depth, cr, width), bf16),
             dma((5,)),
-            dma((6, PIECES)),
+            dma((7, PIECES)),
             dma((5, PIECES)),
             dma((5,)),
             dma((5,)),
@@ -542,9 +624,9 @@
             dma((depth,)),
         ],
         compiler_params=pltpu.CompilerParams(
-            collective_id=0, has_side_effects=True, vmem_limit_bytes=60 * 1024 * 1024
+            collective_id=0, has_side_effects=True, vmem_limit_bytes=52 * 1024 * 1024
         ),
-    )(lengths, history, candidates, users, w_in, w_out)
+    )(*(pltpu.with_memory_space_constraint(x, pltpu.HBM) for x in (lengths, history, candidates, users, w_in, w_out)))
     hbm = pl.BlockSpec(memory_space=pl.ANY)
     return pl.pallas_call(
         hand_out,
@@ -552,9 +634,10 @@
             jax.ShapeDtypeStruct((rows, width), bf16),
             jax.ShapeDtypeStruct((cr, width), bf16),
         ),
-        in_specs=[hbm],
+        in_specs=[vmem],
         out_specs=(hbm, hbm),
-        scratch_shapes=[pltpu.VMEM((rows + cr, width), bf16), dma((2,))],
+        scratch_shapes=[dma((2,))],
+        compiler_params=pltpu.CompilerParams(vmem_limit_bytes=2 * 1024 * 1024),
     )(both)
 
 

time: 44.8 us -> 39.3 us (0.88)
  the two profiles are of different devices: /device:TPU:24 before, /device:TPU:0 now
where the time goes in v3:
time: 39.3 us; the launch traced here: 39.2 us
  Pallas kernels  38.5 us (98%)
  between operations  0.64 us (2%)
    pallas_call x1, Pallas kernels, per_device(): pl.pallas_call(functools.partial(kernel, n), out_shape=jax.ShapeDtypeStru...  37.7 us
    pallas_call x1, Pallas kernels, per_device(): pl.pallas_call(hand_out, out_shape=(jax.ShapeDtypeStruct((rows, width), b...  0.81 us

profile of v3, /device:TPU:0, one launch (start us, length us, event | category | flops | bytes accessed | tf_op | source)
XLA Modules:
  0.0 39.2 jit_solution(15354972243267781186)
XLA Ops:
  0.6 37.7 %shard_map.77.both = bf16[272,1024]{1,0:T(8,128)(2,1)S(1)} custom-call(s32[4]{0:T(128)} %lengths_hbm.1, bf16[256,1024]{1,0:T(8,128)(2,1)} %hist_hbm.1, bf16[16,1024]{1,0:T(8,128)(2,1)} %cand_hbm.1, s32[1,16]{1,0:T(1,128)} %bitcast.1, bf16[1,1024,4096]{2,1,0:T(8,128)(2,1)} %w_in_hbm.1, bf16[1,1024,1024]{2,1,0:T(8,128)(2,1)} %w_out_hbm.1), custom_call_target="tpu_custom_call" | custom-call | tf_op jit(solution)/shard_map/pallas_call | solution.py:589
  38.4 0.8 %shard_map.78 = (bf16[256,1024]{1,0:T(8,128)(2,1)}, bf16[16,1024]{1,0:T(8,128)(2,1)}) custom-call(bf16[272,1024]{1,0:T(8,128)(2,1)S(1)} %shard_map.77.both), custom_call_target="tpu_custom_call" | custom-call | tf_op jit(solution)/shard_map/pallas_call | solution.py:631

commit v4 on v3

--- a/solution.py
+++ b/solution.py
@@ -186,6 +186,7 @@
         (3, xb.at[B2], B5, (s + 3 + p) % n, has_below & has_above & (k == 1), None),
         (4, xb.at[B3], B4, above, has_below & has_above & (r == 0), B3),
         (5, xb.at[B5], B4, partner, (z >= 2) & (r == 3), B5),
+        (7, xb.at[B3], B4, above, has_below & has_above & (r == 1), B3),
         (6, xb.at[B5], B5, sibling, (z >= 2) & (r == 3), B5),
     )
     arrives = {
@@ -218,6 +219,9 @@
         send(0, h, h + 1, None if h < EARLY else p == 0)
         send(1, h, h + 1)
 
+    def routed(kind, h):
+        return {5: h < PIECES - 1, 7: h == PIECES - 1}.get(kind, True)
+
     def hop(buf, h):
         at = pl.ds(h * piece, piece)
 
@@ -225,7 +229,7 @@
         def _():
             pltpu.make_async_copy(hist.at[at], xb.at[buf, at], x_recv.at[buf, h]).wait()
             for kind, src, dst, to, cond, source in moves:
-                if source == buf:
+                if source == buf and routed(kind, h):
 
                     @pl.when(cond)
                     def _():
@@ -405,6 +409,7 @@
                 only(0, hop, B3, h)
         if e == 3:
             only(1, hop, B2, 2)
+            only(1, send, 3, 0, 1)
             only(0, hop, B2, 3)
             only(0, send, 3, 0, PIECES)
         if e == 4:
@@ -414,18 +419,18 @@
                 only(0, hop, B3, h)
             if depth > 1:
                 only(1, c_round, 1)
-            only(1, send, 3, 0, PIECES // 2)
+            only(1, send, 3, 1, PIECES - 1)
         if e == 5:
             if depth > 2:
-                only(3, c_round, 2)
-            only(1, send, 3, PIECES // 2, PIECES)
+                only(1, c_round, 2)
+            only(1, send, 3, PIECES - 1, PIECES)
             only(3, hop, B5, 0)
             only(3, hop, B5, 1)
         if e == 6:
             only(3, c_last)
             only(3, c_scores)
-            if depth > 2:
-                only(2, c_round, 2)
+            only(2, c_last)
+            only(2, c_scores)
             for h in (0, 1):
                 only(2, hop, B5, h)
                 only(1, hop, B3, h)
@@ -433,8 +438,6 @@
                 only(0, hop, B5, h)
             late(1)
         if e == 7:
-            only(2, c_last)
-            only(2, c_scores)
             late(0)
 
     def late(core):
@@ -454,16 +457,17 @@
         3: 1 + SIB + 1,
         4: 1 + 2,
         5: 1 + SIB + 2,
-        6: 1 + 3,
-        7: 1 + 4,
-        8: 1 + SIB + 3,
+        6: 0,
+        7: 1 + 3,
+        8: 1 + 4,
+        9: 1 + SIB + 3,
     }
 
     def live(t):
         return z >= jnp.minimum(t, 1) * (1 - p) + t // 3
 
     def one(e, carry):
-        for at in range(9):
+        for at in range(8):
 
             @pl.when(e == at)
             def _():
@@ -488,10 +492,10 @@
             pl.when((t == 4) & (k == 0))(lambda: swap_half(4).start())
 
         a = pick(e, att_table) - 1
-        ta = a % SIB
-        side = a // SIB
-
-        @pl.when(live(ta) & ((ta < 4) | (k == 0)) & ((ta > 0) | (side < 1) | (k == 1)))
+        ta = (a + SIB) % SIB
+        side = (a + SIB) // SIB - 1
+
+        @pl.when((a >= 0) & live(ta) & ((ta < 4) | (k == 0)) & ((ta > 0) | (side < 1) | (k == 1)))
         def _():
             pl.when((side == 1) & ((ta < 3) | (k == 0)))(lambda: swap_copy(ta).wait_recv())
 
@@ -504,7 +508,7 @@
 
         return carry
 
-    lax.fori_loop(0, 9, one, 0)
+    lax.fori_loop(0, 10, one, 0)
 
     w_copies[4].wait()
 
@@ -512,27 +516,38 @@
         red_wait(d)
         return c + buf3[d].astype(f32)
 
-    @pl.when(p == 0)
-    def _():
-        red_wait(0)
-
-    @pl.when(p == 1)
-    def _():
-        buf3[0] = out3[z, pl.ds(cr, cr)]
-
-    cattn = lax.fori_loop(1, depth, take, buf3[0].astype(f32))
-    y_c = (layer_norm(cattn) * u_s[pl.ds(rows, cr)].astype(f32)).astype(bf16)
-    y = (layer_norm(acc[...]) * u_s[pl.ds(0, rows)].astype(f32)).astype(bf16)
-    both = dot(jnp.concatenate([y, y_c], axis=0), w_out[...])
-    out_ref[pl.ds(0, rows)] = (hist[...].astype(f32) + both[:rows]).astype(bf16)
-    out_ref[pl.ds(rows, cr)] = (cand[...].astype(f32) + both[rows:]).astype(bf16)
+    def cand_rows():
+        pl.when(p == 0)(lambda: red_wait(0))
+
+        @pl.when(p == 1)
+        def _():
+            buf3[0] = out3[z, pl.ds(cr, cr)]
+
+        cattn = lax.fori_loop(1, depth, take, buf3[0].astype(f32))
+        return (layer_norm(cattn) * u_s[pl.ds(rows, cr)].astype(f32)).astype(bf16)
+
+    def event_rows():
+        return (layer_norm(acc[...]) * u_s[pl.ds(0, rows)].astype(f32)).astype(bf16)
+
+    @pl.when(z < depth // 2)
+    def _():
+        out_ref[pl.ds(0, rows)] = (hist[...].astype(f32) + dot(event_rows(), w_out[...])).astype(bf16)
+        out_ref[pl.ds(rows, cr)] = (cand[...].astype(f32) + dot(cand_rows(), w_out[...])).astype(bf16)
+
+    @pl.when(z >= depth // 2)
+    def _():
+        y_c = cand_rows()
+        both = dot(jnp.concatenate([event_rows(), y_c], axis=0), w_out[...])
+        out_ref[pl.ds(0, rows)] = (hist[...].astype(f32) + both[:rows]).astype(bf16)
+        out_ref[pl.ds(rows, cr)] = (cand[...].astype(f32) + both[rows:]).astype(bf16)
 
     for h in range(PIECES):
         for kind, src, dst, to, cond, _ in moves:
-
-            @pl.when(cond)
-            def _():
-                x_copy(src, dst, h, kind, to).wait_send()
+            if routed(kind, h):
+
+                @pl.when(cond)
+                def _():
+                    x_copy(src, dst, h, kind, to).wait_send()
 
     for t, cond in ((0, (k == 0) | (p == 1)), (1, live(1)), (2, live(2)), (3, live(3) & (k == 1))):
 
@@ -612,7 +627,7 @@
             pltpu.VMEM((depth, 2 * cr, width), bf16),
             pltpu.VMEM((depth, cr, width), bf16),
             dma((5,)),
-            dma((7, PIECES)),
+            dma((8, PIECES)),
             dma((5, PIECES)),
             dma((5,)),
             dma((5,)),

time: 39.3 us -> 37.7 us (0.959)
  Pallas kernels: 38.5 us -> 36.9 us
    pallas_call x1, Pallas kernels: 37.7 us -> 36 us  [per_device(): pl.pallas_call(functools.partial(kernel, n), out_shape=jax.ShapeDtypeStru...]
where the time goes in v4:
time: 37.7 us; the launch traced here: 37.5 us
  Pallas kernels  36.9 us (98%)
  between operations  0.64 us (2%)
    pallas_call x1, Pallas kernels, per_device(): pl.pallas_call(functools.partial(kernel, n), out_shape=jax.ShapeDtypeStru...  36 us
    pallas_call x1, Pallas kernels, per_device(): pl.pallas_call(hand_out, out_shape=(jax.ShapeDtypeStruct((rows, width), b...  0.81 us

profile of v4, /device:TPU:0, one launch (start us, length us, event | category | flops | bytes accessed | tf_op | source)
XLA Modules:
  0.0 37.5 jit_solution(12480592114086584498)
XLA Ops:
  0.6 36.0 %shard_map.77.both = bf16[272,1024]{1,0:T(8,128)(2,1)S(1)} custom-call(s32[4]{0:T(128)} %lengths_hbm.1, bf16[256,1024]{1,0:T(8,128)(2,1)} %hist_hbm.1, bf16[16,1024]{1,0:T(8,128)(2,1)} %cand_hbm.1, s32[1,16]{1,0:T(1,128)} %bitcast.1, bf16[1,1024,4096]{2,1,0:T(8,128)(2,1)} %w_in_hbm.1, bf16[1,1024,1024]{2,1,0:T(8,128)(2,1)} %w_out_hbm.1), custom_call_target="tpu_custom_call" | custom-call | tf_op jit(solution)/shard_map/pallas_call | solution.py:604
  36.7 0.8 %shard_map.78 = (bf16[256,1024]{1,0:T(8,128)(2,1)}, bf16[16,1024]{1,0:T(8,128)(2,1)}) custom-call(bf16[272,1024]{1,0:T(8,128)(2,1)S(1)} %shard_map.77.both), custom_call_target="tpu_custom_call" | custom-call | tf_op jit(solution)/shard_map/pallas_call | solution.py:646

commit v5 on v4

--- a/solution.py
+++ b/solution.py
@@ -105,7 +105,13 @@
     in_copies = [
         pltpu.make_async_copy(src, dst, in_sem.at[i])
         for i, (src, dst) in enumerate(
-            ((hist_hbm, hist), (cand_hbm, cand), (users_hbm, users_row), (lengths_hbm, lengths))
+            (
+                (hist_hbm.at[pl.ds(0, piece)], hist.at[pl.ds(0, piece)]),
+                (hist_hbm.at[pl.ds(piece, rows - piece)], hist.at[pl.ds(piece, rows - piece)]),
+                (cand_hbm, cand),
+                (users_hbm, users_row),
+                (lengths_hbm, lengths),
+            )
         )
     ]
     for c in in_copies:
@@ -138,7 +144,22 @@
 
     for c in (3, 1, 2, 0, 4):
         w_copies[c].start()
-    for c in in_copies[1:]:
+    def norm_rows(first, count):
+        at = pl.ds(first, count)
+        own[at] = layer_norm(hist[at].astype(f32)).astype(bf16)
+
+    in_copies[0].wait()
+    norm_rows(0, piece)
+
+    @pl.when((p == 1) & (z == 0))
+    def _():
+        xb[B2] = jnp.zeros((rows, width), bf16)
+
+    @pl.when((p == 1) & (k == 0) & (z == 1))
+    def _():
+        xb[B5] = jnp.zeros((rows, width), bf16)
+
+    for c in in_copies[2:]:
         c.wait()
 
     eye = lax.broadcasted_iota(jnp.int32, (cr, cr), 0) == lax.broadcasted_iota(jnp.int32, (cr, cr), 1)
@@ -150,18 +171,6 @@
     @pl.when(p == 1)
     def _():
         cbuf[z, pl.ds(cr, cr)] = cmsg[...]
-
-    in_copies[0].wait()
-    normed = layer_norm(hist[...].astype(f32)).astype(bf16)
-    own[...] = normed
-
-    @pl.when((p == 1) & (z == 0))
-    def _():
-        xb[B2] = jnp.zeros((rows, width), bf16)
-
-    @pl.when((p == 1) & (k == 0) & (z == 1))
-    def _():
-        xb[B5] = jnp.zeros((rows, width), bf16)
 
     pl.semaphore_wait(barrier, sum(1 if cond is None else cond.astype(jnp.int32) for cond, _ in peers))
 
@@ -183,7 +192,8 @@
         (0, own, B2, above, has_above, None),
         (1, own, B1, partner, p == 0, None),
         (2, xb.at[B2], B3, partner, has_below, B2),
-        (3, xb.at[B2], B5, (s + 3 + p) % n, has_below & has_above & (k == 1), None),
+        (3, xb.at[B2], B5, (s + 4) % n, has_below & has_above & (r == 3), None),
+        (8, xb.at[B2], B5, (s + 3) % n, has_below & has_above & (r == 1), B2),
         (4, xb.at[B3], B4, above, has_below & has_above & (r == 0), B3),
         (5, xb.at[B5], B4, partner, (z >= 2) & (r == 3), B5),
         (7, xb.at[B3], B4, above, has_below & has_above & (r == 1), B3),
@@ -203,10 +213,6 @@
     def c_block(block, send, to):
         return remote(cbuf.at[block], cbuf.at[block], send, c_recv.at[block], to)
 
-    @pl.when(p == 0)
-    def _():
-        c_cross().start()
-
     def send(which, first, last, also=None):
         kind, src, dst, to, cond, _ = moves[which]
 
@@ -215,12 +221,23 @@
             for h in range(first, last):
                 x_copy(src, dst, h, kind, to).start()
 
-    for h in range(PIECES):
+    def own_out(h):
         send(0, h, h + 1, None if h < EARLY else p == 0)
         send(1, h, h + 1)
 
+    @pl.when(p == 0)
+    def _():
+        c_cross().start()
+
+    own_out(0)
+    in_copies[1].wait()
+    norm_rows(piece, rows - piece)
+    for h in range(1, PIECES):
+        own_out(h)
+    normed = own[...]
+
     def routed(kind, h):
-        return {5: h < PIECES - 1, 7: h == PIECES - 1}.get(kind, True)
+        return {5: h < PIECES // 2, 7: h >= PIECES // 2}.get(kind, True)
 
     def hop(buf, h):
         at = pl.ds(h * piece, piece)
@@ -306,27 +323,26 @@
     def _():
         swap_copy(0).start()
 
-    def c_round(d):
+    def c_down(d):
+        high = jnp.minimum(z + d, depth - 1)
+
+        @pl.when(z + d < depth)
+        def _():
+            c_block(high, down_send.at[d], below).wait_recv()
+            pl.when(has_below)(lambda: c_block(high, down_send.at[d], below).start())
+
+    def c_up(d):
         low = jnp.maximum(z - d, 0)
-        high = jnp.minimum(z + d, depth - 1)
-        if isinstance(d, int) and d == 0:
-            pl.when(has_above)(lambda: c_block(z, up_send.at[d], above).start())
-            pl.when(has_below)(lambda: c_block(z, down_send.at[d], below).start())
-            return
 
         @pl.when(z - d >= 0)
         def _():
             c_block(low, up_send.at[d], above).wait_recv()
             pl.when(has_above)(lambda: c_block(low, up_send.at[d], above).start())
 
-        @pl.when(z + d < depth)
-        def _():
-            c_block(high, down_send.at[d], below).wait_recv()
-            pl.when(has_below)(lambda: c_block(high, down_send.at[d], below).start())
-
     def c_first():
         c_cross().wait_recv()
-        c_round(0)
+        pl.when(has_below)(lambda: c_block(z, down_send.at[0], below).start())
+        pl.when(has_above)(lambda: c_block(z, up_send.at[0], above).start())
 
     w_copies[2].wait()
     q_s[...] = project(normed, 2)
@@ -341,7 +357,8 @@
 
     def c_last():
         def rest(d, carry):
-            c_round(d)
+            c_down(d)
+            c_up(d)
             return carry
 
         lax.fori_loop(3, depth, rest, 0)
@@ -411,26 +428,28 @@
             only(1, hop, B2, 2)
             only(1, send, 3, 0, 1)
             only(0, hop, B2, 3)
-            only(0, send, 3, 0, PIECES)
         if e == 4:
+            if depth > 1:
+                only(1, c_down, 1)
+                only(1, c_up, 1)
             only(1, hop, B2, 3)
             for h in (2, 3):
                 hop(B1, h)
                 only(0, hop, B3, h)
-            if depth > 1:
-                only(1, c_round, 1)
             only(1, send, 3, 1, PIECES - 1)
         if e == 5:
             if depth > 2:
-                only(1, c_round, 2)
+                only(1, c_down, 2)
+                only(1, c_up, 2)
             only(1, send, 3, PIECES - 1, PIECES)
             only(3, hop, B5, 0)
             only(3, hop, B5, 1)
         if e == 6:
-            only(3, c_last)
-            only(3, c_scores)
-            only(2, c_last)
-            only(2, c_scores)
+            @pl.when(p == 1)
+            def _():
+                c_last()
+                c_scores()
+
             for h in (0, 1):
                 only(2, hop, B5, h)
                 only(1, hop, B3, h)
@@ -529,49 +548,54 @@
     def event_rows():
         return (layer_norm(acc[...]) * u_s[pl.ds(0, rows)].astype(f32)).astype(bf16)
 
-    @pl.when(z < depth // 2)
+    @pl.when(has_above)
     def _():
         out_ref[pl.ds(0, rows)] = (hist[...].astype(f32) + dot(event_rows(), w_out[...])).astype(bf16)
+
+    for h in range(PIECES):
+        for kind, src, dst, to, cond, _ in moves:
+            if routed(kind, h):
+
+                @pl.when(cond)
+                def _():
+                    x_copy(src, dst, h, kind, to).wait_send()
+
+    for t, cond in ((0, (k == 0) | (p == 1)), (1, live(1)), (2, live(2)), (3, live(3) & (k == 1))):
+
+        @pl.when(cond)
+        def _():
+            swap_copy(t).wait_send()
+
+    @pl.when(live(3) & (k == 0))
+    def _():
+        swap_half(3).wait_send()
+        swap_half(4).wait_send()
+
+    pl.when(p == 0)(lambda: c_cross().wait_send())
+
+    @pl.when(p == 1)
+    def _():
+        def left(d, c):
+            pl.when(has_above & (z - d >= 0))(lambda: c_block(0, up_send.at[d], above).wait_send())
+            pl.when(has_below & (z + d < depth))(lambda: c_block(0, down_send.at[d], below).wait_send())
+            return c
+
+        lax.fori_loop(0, depth, left, 0)
+
+    @pl.when(has_above)
+    def _():
         out_ref[pl.ds(rows, cr)] = (cand[...].astype(f32) + dot(cand_rows(), w_out[...])).astype(bf16)
 
-    @pl.when(z >= depth // 2)
+    @pl.when(z + 1 == depth)
     def _():
         y_c = cand_rows()
         both = dot(jnp.concatenate([event_rows(), y_c], axis=0), w_out[...])
         out_ref[pl.ds(0, rows)] = (hist[...].astype(f32) + both[:rows]).astype(bf16)
         out_ref[pl.ds(rows, cr)] = (cand[...].astype(f32) + both[rows:]).astype(bf16)
 
-    for h in range(PIECES):
-        for kind, src, dst, to, cond, _ in moves:
-            if routed(kind, h):
-
-                @pl.when(cond)
-                def _():
-                    x_copy(src, dst, h, kind, to).wait_send()
-
-    for t, cond in ((0, (k == 0) | (p == 1)), (1, live(1)), (2, live(2)), (3, live(3) & (k == 1))):
-
-        @pl.when(cond)
-        def _():
-            swap_copy(t).wait_send()
-
-    @pl.when(live(3) & (k == 0))
-    def _():
-        swap_half(3).wait_send()
-        swap_half(4).wait_send()
-
-    pl.when(p == 0)(lambda: c_cross().wait_send())
-
     @pl.when(p == 1)
     def _():
         red(0, 0).wait_send()
-
-        def left(d, c):
-            pl.when(has_above & (z - d >= 0))(lambda: c_block(0, up_send.at[d], above).wait_send())
-            pl.when(has_below & (z + d < depth))(lambda: c_block(0, down_send.at[d], below).wait_send())
-            return c
-
-        lax.fori_loop(0, depth, left, 0)
 
         def sums(d, c):
             for side in range(2):
@@ -611,7 +635,7 @@
             pltpu.VMEM((rows, width), bf16),
             pltpu.VMEM((cr, width), bf16),
             pltpu.VMEM((1, cr), jnp.int32),
-            dma((4,)),
+            dma((5,)),
             pltpu.VMEM((4, width, width), bf16),
             pltpu.VMEM((width, width), bf16),
             pltpu.VMEM((rows, width), bf16),
@@ -627,7 +651,7 @@
             pltpu.VMEM((depth, 2 * cr, width), bf16),
             pltpu.VMEM((depth, cr, width), bf16),
             dma((5,)),
-            dma((8, PIECES)),
+            dma((9, PIECES)),
             dma((5, PIECES)),
             dma((5,)),
             dma((5,)),

time: 37.7 us -> 37.2 us (0.987)
  Pallas kernels: 36.9 us -> 36.4 us
    pallas_call x1, Pallas kernels: 36 us -> 35.6 us  [per_device(): pl.pallas_call(functools.partial(kernel, n), out_shape=jax.ShapeDtypeStru...]
where the time goes in v5:
time: 37.2 us; the launch traced here: 37.1 us
  Pallas kernels  36.4 us (98%)
  between operations  0.64 us (2%)
    pallas_call x1, Pallas kernels, per_device(): pl.pallas_call(functools.partial(kernel, n), out_shape=jax.ShapeDtypeStru...  35.6 us
    pallas_call x1, Pallas kernels, per_device(): pl.pallas_call(hand_out, out_shape=(jax.ShapeDtypeStruct((rows, width), b...  0.81 us

profile of v5, /device:TPU:0, one launch (start us, length us, event | category | flops | bytes accessed | tf_op | source)
XLA Modules:
  0.0 37.1 jit_solution(8963898252368545148)
XLA Ops:
  0.6 35.6 %shard_map.77.both = bf16[272,1024]{1,0:T(8,128)(2,1)S(1)} custom-call(s32[4]{0:T(128)} %lengths_hbm.1, bf16[256,1024]{1,0:T(8,128)(2,1)} %hist_hbm.1, bf16[16,1024]{1,0:T(8,128)(2,1)} %cand_hbm.1, s32[1,16]{1,0:T(1,128)} %bitcast.1, bf16[1,1024,4096]{2,1,0:T(8,128)(2,1)} %w_in_hbm.1, bf16[1,1024,1024]{2,1,0:T(8,128)(2,1)} %w_out_hbm.1), custom_call_target="tpu_custom_call" | custom-call | tf_op jit(solution)/shard_map/pallas_call | solution.py:628
  36.2 0.8 %shard_map.78 = (bf16[256,1024]{1,0:T(8,128)(2,1)}, bf16[16,1024]{1,0:T(8,128)(2,1)}) custom-call(bf16[272,1024]{1,0:T(8,128)(2,1)S(1)} %shard_map.77.both), custom_call_target="tpu_custom_call" | custom-call | tf_op jit(solution)/shard_map/pallas_call | solution.py:670

commit v6 on v5

--- a/solution.py
+++ b/solution.py
@@ -373,13 +373,13 @@
             part[g] = jnp.zeros((group, width), f32)
 
             def shard(i, carry):
-                for at in (2, 3):
-                    pl.when((r == 3) & (g == 0) & (i == 2 * at - 3))(functools.partial(hop, B5, at))
+                if i % 2:
+                    pl.when((r == 3) & (g == 0))(functools.partial(hop, B5, (i + 3) // 2))
                 t = i // 2
                 side = i % 2
                 a = t + side * SIB
                 b = 2 * t + side * SIB
-                rest = pl.ds(pl.multiple_of((1 - t) * half, half), half)
+                rest = pl.ds((1 - t) * half, half)
                 near = ROW * z + 2 - 2 * t + k + side - 2 * k * side
                 ok = owner == seg(near * rows + lax.broadcasted_iota(jnp.int32, (1, rows), 1)).astype(f32)
                 for h in range(HEADS):
@@ -391,7 +391,8 @@
                     part[g, :, cols] += dot(weight, values)
                 return carry
 
-            lax.fori_loop(0, 4, shard, 0)
+            for i in range(4):
+                shard(i, 0)
             out3[at] = part[g].astype(bf16).reshape(lines, 2 * cr, width)
             return carry
 

time: 37.2 us -> 36.9 us (level)
  the two profiles are of different devices: /device:TPU:0 before, /device:TPU:20 now
where the time goes in v6:
time: 36.9 us; the launch traced here: 36.7 us
  Pallas kernels  36.1 us (98%)
  between operations  0.64 us (2%)
    pallas_call x1, Pallas kernels, per_device(): pl.pallas_call(functools.partial(kernel, n), out_shape=jax.ShapeDtypeStru...  35.2 us
    pallas_call x1, Pallas kernels, per_device(): pl.pallas_call(hand_out, out_shape=(jax.ShapeDtypeStruct((rows, width), b...  0.81 us

profile of v6, /device:TPU:20, one launch (start us, length us, event | category | flops | bytes accessed | tf_op | source)
XLA Modules:
  0.0 36.7 jit_solution(4265732472888903822)
XLA Ops:
  0.6 35.2 %shard_map.77.both = bf16[272,1024]{1,0:T(8,128)(2,1)S(1)} custom-call(s32[4]{0:T(128)} %lengths_hbm.1, bf16[256,1024]{1,0:T(8,128)(2,1)} %hist_hbm.1, bf16[16,1024]{1,0:T(8,128)(2,1)} %cand_hbm.1, s32[1,16]{1,0:T(1,128)} %bitcast.1, bf16[1,1024,4096]{2,1,0:T(8,128)(2,1)} %w_in_hbm.1, bf16[1,1024,1024]{2,1,0:T(8,128)(2,1)} %w_out_hbm.1), custom_call_target="tpu_custom_call" | custom-call | tf_op jit(solution)/shard_map/pallas_call | solution.py:629
  35.9 0.8 %shard_map.78 = (bf16[256,1024]{1,0:T(8,128)(2,1)}, bf16[16,1024]{1,0:T(8,128)(2,1)}) custom-call(bf16[272,1024]{1,0:T(8,128)(2,1)S(1)} %shard_map.77.both), custom_call_target="tpu_custom_call" | custom-call | tf_op jit(solution)/shard_map/pallas_call | solution.py:671
